TPU v7x, 32 devices: a 4x4x1 block of a 4x4x8 slice. The times are simulated.
32 devices in a mesh: batch: 1 (over z), col: 4 (over y), row: 8 (over x, core).
Axes of the slice: x: 4, y: 4, z: 1, core: 2. Of those that a mesh axis runs over, the one named last changes fastest.
The devices are a block of a 4x4x8 slice.
Arguments:
- tokens: bfloat16 [512, 4, 1536], P(('batch', 'row', 'col'))
- mod_vec: float32 [5, 1536], replicated
- w_fc1: bfloat16 [1536, 6144], replicated
- w_fc2: bfloat16 [6144, 1536], replicated
- w_final: bfloat16 [1536, 64], replicated
- conv_in: bfloat16 [3, 3, 16, 512], replicated
- norm_attn: float32 [2, 512], replicated
- w_qkv: bfloat16 [512, 1536], replicated
- w_proj: bfloat16 [512, 512], replicated
- norm0_a: float32 [2, 512], replicated
- conv0_a: bfloat16 [3, 3, 512, 512], replicated
- norm0_b: float32 [2, 512], replicated
- conv0_b: bfloat16 [3, 3, 512, 512], replicated
- upconv_0: bfloat16 [3, 3, 512, 512], replicated
- norm1_a: float32 [2, 512], replicated
- conv1_a: bfloat16 [3, 3, 512, 512], replicated
- norm1_b: float32 [2, 512], replicated
- conv1_b: bfloat16 [3, 3, 512, 512], replicated
- upconv_1: bfloat16 [3, 3, 512, 512], replicated
- norm2_a: float32 [2, 512], replicated
- conv2_a: bfloat16 [3, 3, 512, 256], replicated
- norm2_b: float32 [2, 256], replicated
- conv2_b: bfloat16 [3, 3, 256, 256], replicated
- skip_2: bfloat16 [512, 256], replicated
- upconv_2: bfloat16 [3, 3, 256, 256], replicated
- norm3_a: float32 [2, 256], replicated
- conv3_a: bfloat16 [3, 3, 256, 128], replicated
- norm3_b: float32 [2, 128], replicated
- conv3_b: bfloat16 [3, 3, 128, 128], replicated
- skip_3: bfloat16 [256, 128], replicated
- norm_out: float32 [2, 128], replicated
- conv_out: bfloat16 [3, 3, 128, 3], replicated
Outputs:
- output: float32 [8192, 64, 3], P(('batch', 'row'), 'col')
All inputs are finite; a program needn't handle non-finite values.
Results may differ from a plain program's by a relative error of at most 0.02.
Values are sent between devices in bfloat16 or wider.
A program may use at most 768 MiB of HBM per device.

v0:
```python
import functools
import jax
import jax.numpy as jnp
from jax import lax
from jax.experimental import pallas as pl
from jax.experimental.pallas import tpu as pltpu
from jax.sharding import PartitionSpec as P

GROUPS = 32
LOG2_E = 1.4426950408889634
LANES = 128
BASE = 16
F32, BF16 = jnp.float32, jnp.bfloat16
MESH = pl.DeviceIdType.MESH
VMEM_SPEC = pl.BlockSpec(memory_space=pltpu.VMEM)
MIB = 1 << 20
TOTALS = jax.ShapeDtypeStruct((1, LANES), F32)


def dot(a, b):
    return jnp.dot(a, b, preferred_element_type=F32)


def dot_t(a, b):
    return lax.dot_general(a, b, (((1,), (1,)), ((), ())), preferred_element_type=F32)


def exact_dot(a, b):
    return jnp.dot(a, b, preferred_element_type=F32, precision=lax.Precision.HIGHEST)


def clear(*refs):
    for ref in refs:
        ref[...] = jnp.zeros_like(ref)


def iota(shape, dim):
    return lax.broadcasted_iota(jnp.int32, shape, dim)


def aligned(first, size, unit):
    return pl.ds(pl.multiple_of(first, unit), size)


def layer_norm(v):
    mean = jnp.mean(v, axis=-1, keepdims=True)
    var = jnp.mean(jnp.square(v - mean), axis=-1, keepdims=True)
    return (v - mean) * lax.rsqrt(var + 1e-6)


def silu_of_half(half):
    return half + half * jnp.tanh(half)


class Net:
    def __init__(self, n_row, n_col):
        self.n_row, self.n_col = n_row, n_col
        self.n = n_row * n_col
        self.row, self.col = lax.axis_index('row'), lax.axis_index('col')
        self.strip = self.row * n_col + self.col

    def for_others(self, act, row_step=1):
        cols = [lax.rem(self.col + k, self.n_col) for k in range(self.n_col)]
        for col in cols[1:]:
            act({'row': self.row, 'col': col})

        def step(k, carry):
            row = lax.rem(self.row + k * row_step, self.n_row)
            for col in cols:
                act({'row': row, 'col': col})
            return carry
        lax.fori_loop(1, self.n_row // row_step, step, 0)
        return self.n // row_step - 1

    def beside(self, ahead):
        other = lax.rem(self.strip + ahead, self.n)
        return {'row': other // self.n_col, 'col': lax.rem(other, self.n_col)}

    def greet(self):
        barrier = pltpu.get_barrier_semaphore()
        self.for_others(lambda device: pl.semaphore_signal(barrier, inc=1, device_id=device, device_id_type=MESH))

    def all_here(self):
        pl.semaphore_wait(pltpu.get_barrier_semaphore(), self.n - 1)

    def to_others(self, src, recv, sems, row_step=1):
        count = self.for_others(lambda device: send(src, recv.at[self.strip], sems, device).start(), row_step)

        def wait():
            done = recv.at[pl.ds(0, count)]
            for side in range(2):
                pltpu.make_async_copy(done, done, sems.at[side]).wait()
        return wait


def send(src, dst, sems, device):
    return pltpu.make_async_remote_copy(
        src_ref=src, dst_ref=dst, send_sem=sems.at[0], recv_sem=sems.at[1], device_id=device, device_id_type=MESH)


PAIR_SEM = pltpu.SemaphoreType.DMA((2,))


def net_scratch(n, edge_shape=None):
    scratch = [pltpu.VMEM((1, LANES), F32), pltpu.VMEM((n, 1, LANES), F32), PAIR_SEM]
    if edge_shape is not None:
        scratch += [pltpu.VMEM((2,) + edge_shape, BF16), PAIR_SEM, PAIR_SEM]
    return scratch


def exchange(net, stat, stat_ref, recv, sems, tot_ref, sides=None):
    stat_ref[...] = stat
    net.all_here()
    wait = net.to_others(stat_ref, recv, sems)
    side_copies = []
    if sides is not None:
        first, last, top, bottom, hrecv, down_sems, up_sems = sides
        side_copies = [(send(src, hrecv.at[side], pair, net.beside(ahead)), dst, side) for side, (src, dst, pair, ahead)
                       in enumerate(((last, top, down_sems, 1), (first, bottom, up_sems, net.n - 1)))]
    for copy, _, _ in side_copies:
        copy.start()
    recv[net.strip] = stat
    wait()
    tot_ref[...] = jnp.sum(recv[...], axis=0)
    for copy, dst, side in side_copies:
        copy.wait()
        dst[...] = hrecv[side]


def sum_scratch(ch):
    return [pltpu.VMEM((8, ch), F32)] * 2


def comm_params(cid, mib):
    return pltpu.CompilerParams(collective_id=cid, has_side_effects=True, vmem_limit_bytes=mib * MIB)


def mlp_kernel(net_shape, x_ref, mod_ref, w1_ref, w2_ref, wf_ref, o_ref,
               w1_buf, w2_buf, act_ref, acc_ref, tok_ref, mix_ref, recv, w_sems, sems, pass_sems):
    net = Net(*net_shape)
    n_buf, blk = w1_buf.shape[0], w1_buf.shape[2]
    n_cut = w1_ref.shape[1] // blk

    def loads(i):
        part, slot = aligned(i * blk, blk, blk), lax.rem(i, n_buf)
        return [pltpu.make_async_copy(w1_ref.at[:, part], w1_buf.at[slot], w_sems.at[0, slot]),
                pltpu.make_async_copy(w2_ref.at[part], w2_buf.at[slot], w_sems.at[1, slot])]
    for i in range(n_buf - 1):
        for load in loads(i):
            load.start()
    net.greet()
    shift1, scale1, gate1, shift2, scale2 = [mod_ref[pl.ds(i, 1)] for i in range(5)]
    x = x_ref[...].astype(F32)
    act = (layer_norm(x) * (1.0 + scale1) + shift1).astype(BF16)
    act_ref[...] = act
    clear(acc_ref)

    def step(i, carry):
        @pl.when(i + n_buf - 1 < n_cut)
        def _():
            for load in loads(i + n_buf - 1):
                load.start()
        load1, load2 = loads(i)
        slot = lax.rem(i, n_buf)
        load1.wait()
        hid = jax.nn.gelu(dot(act_ref[...], w1_buf[slot]), approximate=True).astype(BF16)
        load2.wait()
        acc_ref[...] += dot(hid, w2_buf[slot])
        return carry
    lax.fori_loop(0, n_cut, step, 0)
    acc = acc_ref[...]
    y = (x + gate1 * acc).astype(BF16)
    fin = (layer_norm(y.astype(F32)) * (1.0 + scale2) + shift2).astype(BF16)
    tok_ref[...] = dot_t(fin, wf_ref[...])
    rows, part = mix_ref.shape[0] // 2, wf_ref.shape[0] // 2
    tok_w = tok_ref.shape[0] // rows
    toks = [tok_ref[pl.ds(j, rows, stride=tok_w), :] for j in range(tok_w)]
    for p in range(2):
        mix_ref[pl.ds(p, rows, stride=2), :] = jnp.concatenate([t[:, p * part:(p + 1) * part] for t in toks], axis=1)
    recv[net.strip] = mix_ref[...].astype(BF16)
    net.all_here()
    net.to_others(recv.at[net.strip], recv, sems, 2)()
    core = lax.rem(net.row, 2)
    copies = []
    for i in range(net.n_row // 2):
        line = recv.at[pl.ds((2 * i + core) * net.n_col, net.n_col)]
        copies.append(send(line, line, pass_sems.at[i], {'row': net.row + 1 - 2 * core, 'col': net.col}))
        copies[-1].start()
    for copy in copies:
        copy.wait()
    o_ref[...] = recv[...]


def mlp(x, tok_w, mod_vec, w_fc1, w_fc2, w_final, net_shape, cid):
    n = net_shape[0] * net_shape[1]
    n_tok, d = x.shape
    hid, patch = w_fc1.shape[1], w_final.shape[1]
    n_buf, blk = 4, 768
    rows = 2 * n_tok // tok_w
    lat = (rows, n_tok * patch // rows)
    hbm = pl.BlockSpec(memory_space=pltpu.HBM)
    return pl.pallas_call(
        functools.partial(mlp_kernel, net_shape),
        out_shape=jax.ShapeDtypeStruct((n,) + lat, BF16),
        in_specs=[VMEM_SPEC, VMEM_SPEC, hbm, hbm, VMEM_SPEC],
        out_specs=VMEM_SPEC,
        scratch_shapes=[pltpu.VMEM((n_buf, d, blk), BF16), pltpu.VMEM((n_buf, blk, d), BF16),
                        pltpu.VMEM(x.shape, BF16), pltpu.VMEM(x.shape, F32),
                        pltpu.VMEM((n_tok, patch), F32), pltpu.VMEM(lat, F32), pltpu.VMEM((n,) + lat, BF16),
                        pltpu.SemaphoreType.DMA((2, n_buf)), PAIR_SEM, pltpu.SemaphoreType.DMA((net_shape[0] // 2, 2))],
        compiler_params=comm_params(cid, 48),
        name='mlp',
    )(x, mod_vec, w_fc1, w_fc2, w_final.T)


def in_group(channel, lane, per):
    return ((channel >= lane * per) & (channel < lane * per + per)).astype(F32)


def group_sums(s1, s2):
    ch = s1.shape[1]
    shape = (ch, LANES)
    both = [exact_dot(s, in_group(iota(shape, 0), iota(shape, 1) - at, ch // GROUPS))
            for s, at in ((s1, 0), (s2, GROUPS))]
    return jnp.sum(both[0] + both[1], axis=0, keepdims=True)


def norm_coefs(tot, norm_ref, ch, count):
    avg = jnp.broadcast_to(tot / count, (8, LANES))
    shape = (LANES, ch)
    mean, square = [exact_dot(avg, in_group(iota(shape, 1), iota(shape, 0) - at, ch // GROUPS)) for at in (0, GROUPS)]
    scale = lax.rsqrt(square - jnp.square(mean) + 1e-6) * norm_ref[0:1]
    return mean[0:1], scale[0:1], norm_ref[1:2]


def fold8(v):
    return jnp.sum(v.reshape(v.shape[0] // 8, 8, v.shape[1]), axis=0)


def attention_kernel(net_shape, lat_ref, win_ref, norm_ref, wqkv_ref, wproj_ref, out_ref, tot_ref,
                     cols_ref, toe_ref, fmap_ref, loc_ref, sc_ref, s1_ref, s2_ref, m_ref, l_ref, acc_ref,
                     stat_ref, recv, sems, *halo_refs):
    net = Net(*net_shape)
    net.greet()
    rows = lat_ref.shape[0]
    lat_c, ch = win_ref.shape[1:]
    wid = lat_ref.shape[1] // lat_c
    own = rows // net.n
    lat = lat_ref[...].astype(F32)
    idx = iota(lat.shape, 0)
    cols_ref[...] = jnp.concatenate([jnp.where(idx == 0, 0.0, pltpu.roll(lat, 1, 0)), lat,
                                     jnp.where(idx == rows - 1, 0.0, pltpu.roll(lat, rows - 1, 0))], axis=1).astype(BF16)
    clear(toe_ref)
    for x in range(wid):
        for tap in range(9):
            src = x + tap % 3 - 1
            if 0 <= src < wid:
                toe_ref[x, pl.ds(tap // 3 * LANES + src * lat_c, lat_c), :] = win_ref[tap]
    clear(s1_ref, s2_ref)
    blk = 256
    per_col = rows // blk

    def conv_step(i, carry):
        y = dot(cols_ref[aligned(lax.rem(i, per_col) * blk, blk, blk), :], toe_ref[i // per_col]).astype(BF16)
        fmap_ref[aligned(i * blk, blk, blk), :] = y
        yf = y.astype(F32)
        s1_ref[...] += fold8(yf)
        s2_ref[...] += fold8(yf * yf)
        return carry
    lax.fori_loop(0, wid * per_col, conv_step, 0)
    mean, scale, shift = norm_coefs(group_sums(s1_ref[...], s2_ref[...]), norm_ref, ch, float(rows * wid * (ch // GROUPS)))

    for x in range(wid):
        loc_ref[x * own:(x + 1) * own, :] = fmap_ref[aligned(x * rows + net.strip * own, own, own), :]
    nl = ((loc_ref[...].astype(F32) - mean) * scale + shift).astype(BF16)
    q = dot(nl, wqkv_ref[:, :ch]).astype(BF16)
    qk = (dot_t(q, wqkv_ref[:, ch:2 * ch]) * (scale * (float(ch) ** -0.5 * LOG2_E))).astype(BF16)
    nk, n_q, kb = sc_ref.shape
    m_ref[...] = jnp.full_like(m_ref, -jnp.inf)

    def score_step(i, carry):
        s = dot_t(qk, fmap_ref[aligned(i * kb, kb, kb), :])
        sc_ref[i] = s
        m = m_ref[...]
        for j in range(kb // LANES):
            m = jnp.maximum(m, s[:, j * LANES:(j + 1) * LANES])
        m_ref[...] = m
        return carry
    lax.fori_loop(0, nk, score_step, 0)
    m_ref[...] = jnp.broadcast_to(jnp.max(m_ref[...], axis=1, keepdims=True), m_ref.shape)
    clear(l_ref, acc_ref)

    def value_step(i, carry):
        m = m_ref[...]
        tot_l = l_ref[...]
        parts = []
        for j in range(kb // LANES):
            e = jnp.exp2(sc_ref[i, :, j * LANES:(j + 1) * LANES] - m).astype(BF16)
            tot_l = tot_l + e.astype(F32)
            parts.append(e)
        l_ref[...] = tot_l
        acc_ref[...] += dot(jnp.concatenate(parts, axis=1), fmap_ref[aligned(i * kb, kb, kb), :])
        return carry
    lax.fori_loop(0, nk, value_step, 0)
    pn = acc_ref[...] / jnp.sum(l_ref[...], axis=1, keepdims=True)
    pn = ((pn - mean) * scale + shift).astype(BF16)
    att = dot(pn, wqkv_ref[:, 2 * ch:]).astype(BF16)
    out = (loc_ref[...].astype(F32) + dot(att, wproj_ref[...])).astype(BF16)
    i, j = iota((n_q, n_q), 0), iota((n_q, n_q), 1)
    perm = (j == lax.rem(i, wid) * own + i // wid).astype(BF16)
    of = dot(perm, out)
    out_ref[pl.ds(1, own)] = of.astype(BF16).reshape(own, wid, ch)
    exchange(net, group_sums(fold8(of), fold8(of * of)), stat_ref, recv, sems, tot_ref,
             (out_ref.at[1], out_ref.at[own], out_ref.at[0], out_ref.at[own + 1], *halo_refs))


def attention(lat, conv_in, norm, w_qkv, w_proj, net_shape, cid):
    n = net_shape[0] * net_shape[1]
    rows = lat.shape[0]
    lat_c, ch = conv_in.shape[2:]
    wid = lat.shape[1] // lat_c
    own = rows // n
    n_q = own * wid
    kb = 512
    return pl.pallas_call(
        functools.partial(attention_kernel, net_shape),
        out_shape=[jax.ShapeDtypeStruct((own + 2, wid, ch), BF16), TOTALS],
        in_specs=[VMEM_SPEC] * 5, out_specs=[VMEM_SPEC] * 2,
        scratch_shapes=[pltpu.VMEM((rows, 3 * LANES), BF16), pltpu.VMEM((wid, 3 * LANES, ch), BF16),
                        pltpu.VMEM((rows * wid, ch), BF16), pltpu.VMEM((n_q, ch), BF16),
                        pltpu.VMEM((rows * wid // kb, n_q, kb), F32),
                        *sum_scratch(ch),
                        pltpu.VMEM((n_q, LANES), F32), pltpu.VMEM((n_q, LANES), F32), pltpu.VMEM((n_q, ch), F32)]
        + net_scratch(n, (wid, ch)),
        compiler_params=comm_params(cid, 27),
        name='attention',
    )(lat, conv_in.reshape(9, lat_c, ch), norm, w_qkv, w_proj)


def shifted(y, wid, by):
    n_px, ch = y.shape
    if wid > BASE:
        even, odd = jnp.split(y.reshape(n_px // wid, 2, wid // 2, ch), 2, axis=1)
        far = shifted((odd if by == 1 else even).reshape(n_px // 2, ch), wid // 2, by).reshape(even.shape)
        return jnp.concatenate([far, even] if by == 1 else [odd, far], axis=1).reshape(n_px, ch)
    tiles = pltpu.roll(y, by % n_px, 0).reshape(n_px // wid, wid // 8, 8, ch)
    at, sub = (0, 0) if by > 0 else (wid // 8 - 1, 7)
    edge = tiles[:, at:at + 1]
    edge = jnp.where(iota(edge.shape, 2) == sub, 0.0, edge)
    parts = [tiles[:, :at], edge, tiles[:, at + 1:]]
    return jnp.concatenate([p for p in parts if p.shape[1]], axis=1).reshape(n_px, ch)


class Rows:
    def __init__(self, net, x_ref, coefs, wid, h, pad, n_out, blk, pair):
        self.net, self.x_ref, self.coefs, self.wid, self.h, self.pad = net, x_ref, coefs, wid, h, pad
        self.n_out, self.blk, self.pair = n_out, blk, pair
        self.ch = x_ref.shape[-1]

    def inside(self, row):
        net = self.net
        return ((row >= self.pad) | (net.strip > 0)) & ((row < self.h + self.pad) | (net.strip < net.n - 1))

    def fill(self, buf, b, before=None):
        mean, scale, shift = self.coefs
        scale = 0.5 * scale
        shift = 0.5 * shift - mean * scale
        wid, ch, blk = self.wid, self.ch, self.blk
        if before is not None:
            self.keep_last(buf, before)
        together = -(-BASE // wid)
        for j in range(2 * (before is not None), blk + 2, together):
            row = b * blk + j
            if self.n_out > blk:
                row = jnp.minimum(row, self.n_out + 1)
            v = self.x_ref[aligned(row * wid, together * wid, 8), :].astype(F32)
            if together == 1:
                keep = jnp.where(self.inside(row), 1.0, 0.0)
                y = silu_of_half(v * (scale * keep) + shift * keep)
            else:
                y = silu_of_half(v * scale + shift)
                y = jnp.where(self.inside(row + iota(y.shape, 0) // wid), y, 0.0)
            for lane, part in enumerate((shifted(y, wid, 1), y, shifted(y, wid, -1))):
                lanes = slice(lane * ch, (lane + 1) * ch)
                self.put(buf, j, together, lanes, part.astype(buf.dtype))

    def keep_last(self, buf, before):
        wid, blk = self.wid, self.blk
        if self.pair:
            buf[:, :wid, :] = before[:, blk // 2 * wid:, :]
        else:
            buf[:2 * wid, :] = before[blk * wid:, :]

    def put(self, buf, j, together, lanes, part):
        wid = self.wid
        if self.pair:
            buf[j % 2, j // 2 * wid:(j // 2 + 1) * wid, lanes] = part
        else:
            buf[j * wid:(j + together) * wid, lanes] = part

    def buffer(self):
        n_px, ch = (self.blk + 2) * self.wid, self.ch
        shape = (2, n_px // 2, 3 * ch) if self.pair else (n_px, 3 * ch)
        return pltpu.VMEM(shape, F32 if self.wid < 16 else BF16)

    def product(self, buf, w_ref):
        acc = None
        m = self.blk * self.wid // (2 if self.pair else 1)
        for t in range(4 if self.pair else 3):
            if self.pair:
                lhs = buf[t % 2, t // 2 * self.wid:t // 2 * self.wid + m, :]
            else:
                lhs = buf[t * self.wid:t * self.wid + m, :].astype(BF16)
            part = dot(lhs, w_ref[t])
            acc = part if acc is None else acc + part
        return acc

    def run(self, bufs, work):
        n_blk = -(-self.n_out // self.blk)
        self.fill(bufs[0], 0)
        if n_blk > 1:
            def step(i, carry):
                self.fill(bufs[1], 2 * i + 1, bufs[0])
                work(bufs[0], 2 * i)
                self.fill(bufs[0], 2 * i + 2, bufs[1])
                work(bufs[1], 2 * i + 1)
                return carry
            lax.fori_loop(0, n_blk // 2, step, 0)
        if n_blk % 2:
            work(bufs[0], n_blk - 1)


def paired_weights(w_ref, wp_ref):
    oc = w_ref.shape[2]
    clear(wp_ref)
    for t in range(3):
        wp_ref[t, :, :oc] = w_ref[t]
        wp_ref[t + 1, :, oc:] = w_ref[t]


def conv_kernel(cfg, *refs):
    net_shape, wid, h, blk, out_ext, pair, shortcut, stats, edge = cfg
    refs = iter(refs)
    x_ref, norm_tot_ref, norm_ref, w_ref = [next(refs) for _ in 'abcd']
    short_ref = next(refs) if shortcut else None
    skip_ref = next(refs) if shortcut == 'matmul' else None
    out_ref = next(refs)
    tot_ref = next(refs) if stats else None
    buf0, buf1, s1_ref, s2_ref = [next(refs) for _ in 'abcd']
    wp_ref = next(refs) if pair else w_ref
    net_refs = list(refs)
    net = Net(*net_shape)
    if stats:
        net.greet()
    ch, oc = x_ref.shape[-1], w_ref.shape[2]
    n_out = h + 2 * out_ext
    coefs = norm_coefs(norm_tot_ref[...], norm_ref, ch, float(net.n * h * wid * (ch // GROUPS)))
    rows = Rows(net, x_ref, coefs, wid, h, 1 + out_ext, n_out, blk, pair)
    clear(s1_ref, s2_ref)
    if pair:
        paired_weights(w_ref, wp_ref)
    exact = n_out % blk == 0 and not out_ext

    def count(y, first_row, step):
        yf = y.astype(F32)
        if exact:
            s1_ref[...] += fold8(yf)
            s2_ref[...] += fold8(yf * yf)
            return
        for i, part in enumerate(jnp.split(yf, yf.shape[0] // wid)):
            r = first_row + step * i
            own = (r >= out_ext) & (r < h + out_ext)
            s1_ref[...] += jnp.where(own, fold8(part), 0.0)
            s2_ref[...] += jnp.where(own, fold8(part * part), 0.0)

    def work(buf, b):
        k0 = b * blk
        acc = rows.product(buf, wp_ref)
        if pair:
            for a in range(2):
                val = acc[:, a * oc:(a + 1) * oc]
                here = pl.ds(edge // 2 + k0 // 2, blk // 2)
                if shortcut:
                    src = short_ref[pl.ds(k0 // 2, blk // 2), a]
                    val = dot(src.reshape(blk // 2 * wid, src.shape[-1]), skip_ref[...]) + val
                y = val.astype(BF16)
                out_ref[here, a] = y.reshape(blk // 2, wid, oc)
                if stats:
                    count(y, k0 + a, 2)
        else:
            if shortcut == 'add':
                acc = short_ref[aligned(k0 * wid, blk * wid, 8), :].astype(F32) + acc
            elif shortcut == 'matmul':
                acc = dot(short_ref[aligned(k0 * wid, blk * wid, 8), :], skip_ref[...]) + acc
            y = acc.astype(BF16)
            out_ref[aligned((k0 + edge) * wid, blk * wid, 8), :] = y
            if stats:
                count(y, k0, 1)
    rows.run((buf0, buf1), work)
    if out_ext:
        for at, at_edge in ((0, net.strip == 0), (n_out - 1, net.strip == net.n - 1)):
            where = out_ref.at[at // 2, at % 2] if pair else out_ref.at[pl.ds(at * wid, wid)]

            @pl.when(at_edge)
            def _():
                where[...] = jnp.zeros(where.shape, BF16)
    if stats:
        sides = None
        if edge:
            def part(row):
                return out_ref.at[row // 2] if pair else out_ref.at[pl.ds(row * wid, edge * wid)]
            sides = (part(edge), part(h), part(0), part(h + edge), *net_refs[3:])
        exchange(net, group_sums(s1_ref[...], s2_ref[...]), *net_refs[:3], tot_ref, sides)


def conv(x, tot, norm, w, h, wid, net_shape, blk, out_ext, stats, edge, pair, cid, *shortcut):
    n = net_shape[0] * net_shape[1]
    ch, oc = w.shape[2:]
    args = [x, tot, norm, w.reshape(3, 3 * ch, oc)]
    for short in shortcut[:1]:
        args.append(short.reshape(-1, 2, wid, short.shape[-1]) if pair else short)
    args += shortcut[1:]
    n_out = h + 2 * out_ext
    rows = -(-n_out // blk) * blk + 2 * edge
    outs = [jax.ShapeDtypeStruct((rows // 2, 2, wid, oc) if pair else (rows * wid, oc), BF16)]
    if stats:
        outs.append(TOTALS)
    cfg = (net_shape, wid, h, blk, out_ext, pair, ('', 'add', 'matmul')[len(shortcut)], stats, edge)
    layout = Rows(None, x, None, wid, h, None, n_out, blk, pair)
    scratch = [layout.buffer(), layout.buffer(), *sum_scratch(oc)]
    if pair:
        scratch.append(pltpu.VMEM((4, 3 * ch, 2 * oc), BF16))
    if stats:
        scratch += net_scratch(n, ((2, wid, oc) if pair else (edge * wid, oc)) if edge else None)
    px = n_out * wid
    res = pl.pallas_call(
        functools.partial(conv_kernel, cfg),
        out_shape=outs, in_specs=[VMEM_SPEC] * len(args), out_specs=[VMEM_SPEC] * len(outs),
        scratch_shapes=scratch,
        compiler_params=comm_params(cid, 28) if stats else pltpu.CompilerParams(vmem_limit_bytes=28 * MIB),
        cost_estimate=pl.CostEstimate(flops=18 * ch * oc * px, bytes_accessed=2 * px * (ch + oc), transcendentals=px * ch),
        name='conv_w%d_%d_%d' % (wid, ch, oc) + ('e' if out_ext else ''),
    )(*args)
    return [res[0].reshape(rows * wid, oc)] + list(res[1:])


def upconv_kernel(cfg, x_ref, w_ref, out_ref, tot_ref, s1_ref, s2_ref, mix_ref, stat_ref, recv, sems):
    net_shape, half, hs, blk = cfg
    net = Net(*net_shape)
    net.greet()
    oc = w_ref.shape[2]
    n_k = hs + 1
    mixed = half < BASE
    m, more = blk * half, (blk + 1) * half
    clear(s1_ref, s2_ref)

    def step(b, carry):
        k0 = jnp.minimum(b * blk, n_k - blk) if n_k > blk else 0
        x = x_ref[aligned(k0 * half, more, 8), :]
        rows = []
        for dx in range(3):
            above, mid, below = [dot(x, w_ref[3 * dy + dx]) for dy in range(3)]
            both = above[:m] + below[half:]
            rows.append((both + mid[:m], both + mid[half:]))
        for a in range(2):
            left, at, right = [r[a] for r in rows]
            even = at + right + shifted(left, half, 1)
            odd = left + at + shifted(right, half, -1)
            for q, val in ((0, even), (1, odd)):
                y = val.astype(BF16)
                if mixed:
                    for c in range(0, oc, LANES):
                        mix_ref[a, c // LANES, pl.ds(q, m, stride=2), :] = val[:, c:c + LANES]
                else:
                    out_ref[pl.ds(k0, blk), a, q * half:(q + 1) * half, :] = y.reshape(blk, half, oc)
                yf = y.astype(F32)
                for i, part in enumerate(jnp.split(yf, blk)):
                    k = k0 + i
                    own = (k >= b * blk) & ((k < hs) if a else (k > 0))
                    s1_ref[...] += jnp.where(own, fold8(part), 0.0)
                    s2_ref[...] += jnp.where(own, fold8(part * part), 0.0)
            for c in range(0, oc if mixed else 0, LANES):
                out_ref[pl.ds(k0, blk), a, :, c:c + LANES] = mix_ref[a, c // LANES].astype(BF16).reshape(blk, 2 * half, LANES)
        return carry
    if n_k == blk:
        step(0, 0)
    else:
        lax.fori_loop(0, -(-n_k // blk), step, 0)
    exchange(net, group_sums(s1_ref[...], s2_ref[...]), stat_ref, recv, sems, tot_ref)


def upconv(x, w, hs, half, net_shape, blk, cid):
    n = net_shape[0] * net_shape[1]
    ch, oc = w.shape[2:]
    n_k = hs + 8
    px = 4 * n_k * half
    out, tot = pl.pallas_call(
        functools.partial(upconv_kernel, (net_shape, half, hs, blk)),
        out_shape=[jax.ShapeDtypeStruct((n_k, 2, 2 * half, oc), BF16), TOTALS],
        in_specs=[VMEM_SPEC] * 2, out_specs=[VMEM_SPEC] * 2,
        scratch_shapes=[*sum_scratch(oc),
                        pltpu.VMEM((2, oc // LANES, 2 * blk * half if half < BASE else 8, LANES), F32)] + net_scratch(n),
        compiler_params=comm_params(cid, 28),
        cost_estimate=pl.CostEstimate(flops=5 * ch * oc * px, bytes_accessed=2 * px * (ch + oc), transcendentals=0),
        name='upconv_w%d' % (2 * half),
    )(x, w.reshape(9, ch, oc))
    return out.reshape(px, oc), tot


class QuarterRows(Rows):
    def keep_last(self, buf, before):
        buf[:, :2 * self.tile] = before[:, self.blk * self.tile:]

    def put(self, buf, j, together, lanes, part):
        n_q = buf.shape[0]
        here = self.tile // (self.wid // BASE)
        whole = part.reshape(self.wid // BASE, BASE, part.shape[1])
        for q in range(n_q):
            buf[q, j * self.tile:(j + 1) * self.tile, lanes] = whole[:, q * here:(q + 1) * here].reshape(self.tile, part.shape[1])


def last_kernel(cfg, x_ref, tot_ref, norm_ref, w_ref, out_ref, buf0, buf1, mine, recv, send_sems, recv_sems):
    net_shape, wid, h, blk, oc = cfg
    net = Net(*net_shape)
    barrier = pltpu.get_barrier_semaphore()
    cols = [lax.rem(net.col + k, net.n_col) for k in range(net.n_col)]
    for col in cols[1:]:
        pl.semaphore_signal(barrier, inc=1, device_id={'col': col}, device_id_type=MESH)
    ch = x_ref.shape[1]
    coefs = norm_coefs(tot_ref[...], norm_ref, ch, float(net.n * h * wid * (ch // GROUPS)))
    rows = QuarterRows(net, x_ref, coefs, wid, h, 1, h, blk, False)
    rows.tile = tile = wid // net.n_col
    m = blk * tile
    per = h * tile // LANES

    def work(buf, b):
        for q in range(net.n_col):
            z = dot_t(w_ref[...], buf[q])
            z = z[:8, :m] + z[8:16, tile:tile + m] + z[16:, 2 * tile:2 * tile + m]
            for c in range(oc):
                for t in range(m // LANES):
                    mine[q, pl.ds(c * per + b * (m // LANES) + t, 1), :] = z[c:c + 1, t * LANES:(t + 1) * LANES]
    rows.run((buf0, buf1), work)
    pl.semaphore_wait(barrier, net.n_col - 1)
    copies = []
    for k, col in enumerate(cols[1:]):
        copies.append(pltpu.make_async_remote_copy(
            src_ref=mine.at[col], dst_ref=recv.at[net.col], send_sem=send_sems.at[k], recv_sem=recv_sems.at[k],
            device_id={'col': col}, device_id_type=MESH))
        copies[-1].start()
    recv[net.col] = mine[net.col]
    for copy in copies:
        copy.wait()
    i, j = iota((LANES, LANES), 0), iota((LANES, LANES), 1)
    splits = wid // BASE
    lane, run = lax.rem(j, tile), j // tile
    src = run * tile + lax.rem(lane, 2) * (tile // 2) + lax.rem(lane // 2, splits // 2) * (tile // splits) + lane // splits
    perm = (i == src).astype(F32)
    for q in range(net.n_col):
        out_ref[q] = exact_dot(recv[q], perm)


def last_conv(x, tot, norm, w, h, wid, net_shape, blk, cid):
    n_col = net_shape[1]
    ch, oc = w.shape[2:]
    wt = jnp.zeros((3, 8, 3 * ch), BF16).at[:, :oc].set(w.reshape(3, 3 * ch, oc).transpose(0, 2, 1))
    buf = pltpu.VMEM((n_col, (blk + 2) * wid // n_col, 3 * ch), BF16)
    shape = (n_col, oc * h * wid // n_col // LANES, LANES)
    return pl.pallas_call(
        functools.partial(last_kernel, (net_shape, wid, h, blk, oc)),
        out_shape=jax.ShapeDtypeStruct(shape, F32),
        in_specs=[VMEM_SPEC] * 4, out_specs=VMEM_SPEC,
        scratch_shapes=[buf, buf, pltpu.VMEM(shape, F32), pltpu.VMEM(shape, F32)] + [pltpu.SemaphoreType.DMA((n_col,))] * 2,
        compiler_params=comm_params(cid, 28),
        name='last_conv',
    )(x, tot, norm, wt.reshape(-1, 3 * ch))


def device_body(net_shape, tokens, mod_vec, w_fc1, w_fc2, w_final, conv_in, norm_attn, w_qkv, w_proj,
                norm0_a, conv0_a, norm0_b, conv0_b, upconv_0, norm1_a, conv1_a, norm1_b, conv1_b, upconv_1,
                norm2_a, conv2_a, norm2_b, conv2_b, skip_2, upconv_2, norm3_a, conv3_a, norm3_b, conv3_b,
                skip_3, norm_out, conv_out):
    n_col = net_shape[1]
    trows, tok_w, d = tokens.shape
    full = mlp(tokens.reshape(-1, d), tok_w, mod_vec, w_fc1, w_fc2, w_final, net_shape, 1)
    h, wid = 2 * trows, 2 * tok_w
    f, tot = attention(full.reshape(-1, full.shape[-1]), conv_in, norm_attn, w_qkv, w_proj, net_shape, 2)
    u = f.reshape(-1, f.shape[-1])
    blocks = [(norm0_a, conv0_a, norm0_b, conv0_b, (), upconv_0, h, h + 2, h + 1),
              (norm1_a, conv1_a, norm1_b, conv1_b, (), upconv_1, 16, 11, 13),
              (norm2_a, conv2_a, norm2_b, conv2_b, (skip_2,), upconv_2, 8, 10, 10),
              (norm3_a, conv3_a, norm3_b, conv3_b, (skip_3,), None, 8, 16, 0)]
    cid = 3
    for norm_a, conv_a, norm_b, conv_b, skip, up, blk_a, blk_b, blk_up in blocks:
        last = up is None
        g, tot = conv(u, tot, norm_a, conv_a, h, wid, net_shape, blk_a, 0, True, 2, last, cid)
        f, *tot = conv(g, tot, norm_b, conv_b, h, wid, net_shape, blk_b, 1, last, 0, last, cid + 1, u, *skip)
        if not last:
            u, tot = upconv(f, up, h, wid, net_shape, blk_up, cid + 2)
            h, wid = 2 * h, 2 * wid
        cid += 3
    tile = last_conv(f, tot[0], norm_out, conv_out, h, wid, net_shape, 16, cid)
    tile = tile.reshape(n_col, -1, h, wid // n_col).transpose(0, 2, 3, 1)
    return tile.reshape(n_col * h, wid // n_col, -1)


def solution(mesh):
    body_fn = functools.partial(device_body, (mesh.shape['row'], mesh.shape['col']))
    tok_spec = P(('batch', 'row', 'col'), None, None)
    out_spec = P(('batch', 'row'), 'col', None)
    return jax.shard_map(body_fn, mesh=mesh, in_specs=(tok_spec,) + (P(),) * 31, out_specs=out_spec, check_vma=False)
```

profile of v0, /device:TPU:97, one launch (start us, length us, event | category | flops | bytes accessed | tf_op | source)
XLA Modules:
  0.0 212.4 jit_solution(669477213395397915)
XLA Ops:
  0.0 1.0 reshape.104.x_ref
  1.0 0.0 slice-start
  1.0 0.0 copy-start.3
  1.0 1.1 copy-done.3
  2.1 1.1 copy-done.5
  3.1 0.0 copy-start
  3.2 0.0 copy-start.8
  3.2 25.4 %mlp.1 = bf16[32,32,128]{2,1,0:T(8,128)(2,1)S(1)} custom-call(bf16[64,1536]{1,0:T(8,128)(2,1)S(1)} %reshape.104.x_ref, f32[5,1536]{1,0:T(8,128)S(1)} %copy-done.5, bf16[1536,6144]{1,0:T(8,128)(2,1)} %w1_ref.1, bf16[6144,1536]{1,0:T(8,128)(2,1)} %w2_ref.1, bf16[64,1536]{1,0:T(8,128)(2,1)S(1)} %bitcast.36), custom_call_target="tpu_custom_call" | custom-call | tf_op jit(solution)/shard_map/mlp/pallas_call | solution.py:202
  28.6 0.0 copy-start.7
  28.6 0.0 slice-start.2
  28.6 28.5 %attention.1 = (bf16[34,8,512]{2,1,0:T(8,128)(2,1)S(1)}, f32[1,128]{1,0:T(1,128)S(1)}) custom-call(bf16[1024,128]{1,0:T(8,128)(2,1)S(1)} %bitcast.35, bf16[9,16,512]{2,1,0:T(8,128)(2,1)S(1)} %bitcast.37, f32[2,512]{1,0:T(2,128)S(1)} %copy-done.6, bf16[512,1536]{1,0:T(8,128)(2,1)S(1)} %copy-done.1, bf16[512,512]{1,0:T(8,128)(2,1)S(1)} %copy-done.2), custom_call_target="tpu_custom_call" | custom-call | tf_op jit(solution)/shard_map/attention/pallas_call | solution.py:325
  57.2 0.0 slice-start.3
  57.2 0.0 slice-start.4
  57.2 8.5 %conv_w8_512_512.1 = (bf16[288,512]{1,0:T(8,128)(2,1)S(1)}, f32[1,128]{1,0:T(1,128)S(1)}) custom-call(bf16[272,512]{1,0:T(8,128)(2,1)S(1)} %bitcast.33, f32[1,128]{1,0:T(1,128)S(1)} %get-tuple-element.36.refs_1_, f32[2,512]{1,0:T(2,128)S(1)} %copy-done.8, bf16[3,1536,512]{2,1,0:T(8,128)(2,1)S(1)} %bitcast.28), custom_call_target="tpu_custom_call" | custom-call | flops 1207959552 | bytes 524288 | tf_op jit(solution)/shard_map/conv_w8_512_512/pallas_call | solution.py:536
  65.7 0.0 slice-start.5
  65.7 2.2 %conv_w8_512_512e.1.x_ref = bf16[272,512]{1,0:T(8,128)(2,1)S(1)} custom-call(bf16[288,512]{1,0:T(8,128)(2,1)S(1)} %get-tuple-element.37.refs_0_, f32[1,128]{1,0:T(1,128)S(1)} %get-tuple-element.38.refs_1_, f32[2,512]{1,0:T(2,128)S(1)} %copy-done.7, bf16[3,1536,512]{2,1,0:T(8,128)(2,1)S(1)} %bitcast.31, bf16[272,512]{1,0:T(8,128)(2,1)S(1)} %bitcast.34), custom_call_target="tpu_custom_call" | custom-call | flops 1283457024 | bytes 557056 | tf_op jit(solution)/shard_map/conv_w8_512_512e/pallas_call | solution.py:536
  67.9 0.0 copy-start.17
  67.9 0.0 slice-start.6
  67.9 8.8 %upconv_w16.1 = (bf16[40,2,16,512]{3,2,1,0:T(8,128)(2,1)S(1)}, f32[1,128]{1,0:T(1,128)S(1)}) custom-call(bf16[272,512]{1,0:T(8,128)(2,1)S(1)} %conv_w8_512_512e.1.x_ref, bf16[9,512,512]{2,1,0:T(8,128)(2,1)S(1)} %bitcast.40), custom_call_target="tpu_custom_call" | custom-call | flops 1677721600 | bytes 2621440 | tf_op jit(solution)/shard_map/upconv_w16/pallas_call | solution.py:597
  76.8 0.0 slice-start.7
  76.8 0.0 copy-start.18
  76.8 0.0 slice-start.8
  76.8 12.1 %conv_w16_512_512.1 = (bf16[1088,512]{1,0:T(8,128)(2,1)S(1)}, f32[1,128]{1,0:T(1,128)S(1)}) custom-call(bf16[1280,512]{1,0:T(8,128)(2,1)S(1)} %bitcast.59, f32[1,128]{1,0:T(1,128)S(1)} %get-tuple-element.40.refs_1_, f32[2,512]{1,0:T(2,128)S(1)} %copy-done.17, bf16[3,1536,512]{2,1,0:T(8,128)(2,1)S(1)} %bitcast.43), custom_call_target="tpu_custom_call" | custom-call | flops 4831838208 | bytes 2097152 | tf_op jit(solution)/shard_map/conv_w16_512_512/pallas_call | solution.py:536
  88.9 0.0 slice-start.9
  89.0 6.8 %conv_w16_512_512e.1.x_ref = bf16[1056,512]{1,0:T(8,128)(2,1)S(1)} custom-call(bf16[1088,512]{1,0:T(8,128)(2,1)S(1)} %get-tuple-element.41.refs_0_, f32[1,128]{1,0:T(1,128)S(1)} %get-tuple-element.42.refs_1_, f32[2,512]{1,0:T(2,128)S(1)} %copy-done.18, bf16[3,1536,512]{2,1,0:T(8,128)(2,1)S(1)} %bitcast.46, bf16[1280,512]{1,0:T(8,128)(2,1)S(1)} %bitcast.60), custom_call_target="tpu_custom_call" | custom-call | flops 4982833152 | bytes 2162688 | tf_op jit(solution)/shard_map/conv_w16_512_512e/pallas_call | solution.py:536
  95.7 0.0 copy-start.10
  95.8 0.0 copy-start.19
  95.8 15.6 %upconv_w32.1 = (bf16[72,2,32,512]{3,2,1,0:T(8,128)(2,1)S(1)}, f32[1,128]{1,0:T(1,128)S(1)}) custom-call(bf16[1056,512]{1,0:T(8,128)(2,1)S(1)} %conv_w16_512_512e.1.x_ref, bf16[9,512,512]{2,1,0:T(8,128)(2,1)S(1)} %bitcast.49), custom_call_target="tpu_custom_call" | custom-call | flops 6039797760 | bytes 9437184 | tf_op jit(solution)/shard_map/upconv_w32/pallas_call | solution.py:597
  111.4 0.0 copy-start.11
  111.4 0.0 copy-start.15
  111.5 0.0 copy-start.20
  111.5 18.1 %conv_w32_512_256.1 = (bf16[4224,256]{1,0:T(8,128)(2,1)S(1)}, f32[1,128]{1,0:T(1,128)S(1)}) custom-call(bf16[4608,512]{1,0:T(8,128)(2,1)S(1)} %bitcast.56, f32[1,128]{1,0:T(1,128)S(1)} %get-tuple-element.44.refs_1_, f32[2,512]{1,0:T(2,128)S(1)} %copy-done.19, bf16[3,1536,256]{2,1,0:T(8,128)(2,1)S(1)} %bitcast.50), custom_call_target="tpu_custom_call" | custom-call | flops 9663676416 | bytes 6291456 | tf_op jit(solution)/shard_map/conv_w32_512_256/pallas_call | solution.py:536
  129.6 0.0 copy-start.12
  129.6 8.2 %conv_w32_256_256e.1.x_ref = bf16[4160,256]{1,0:T(8,128)(2,1)S(1)} custom-call(bf16[4224,256]{1,0:T(8,128)(2,1)S(1)} %get-tuple-element.45.refs_0_, f32[1,128]{1,0:T(1,128)S(1)} %get-tuple-element.46.refs_1_, f32[2,256]{1,0:T(2,128)S(1)} %copy-done.20, bf16[3,768,256]{2,1,0:T(8,128)(2,1)S(1)} %bitcast.51, bf16[4608,512]{1,0:T(8,128)(2,1)S(1)} %bitcast.57, ...), custom_call_target="tpu_custom_call" | custom-call | flops 4907335680 | bytes 4259840 | tf_op jit(solution)/shard_map/conv_w32_256_256e/pallas_call | solution.py:536
  137.8 0.0 copy-start.13
  137.8 0.0 copy-start.21
  137.8 17.6 %upconv_w64.1 = (bf16[136,2,64,256]{3,2,1,0:T(8,128)(2,1)S(1)}, f32[1,128]{1,0:T(1,128)S(1)}) custom-call(bf16[4160,256]{1,0:T(8,128)(2,1)S(1)} %conv_w32_256_256e.1.x_ref, bf16[9,256,256]{2,1,0:T(8,128)(2,1)S(1)} %bitcast.52), custom_call_target="tpu_custom_call" | custom-call | flops 5704253440 | bytes 17825792 | tf_op jit(solution)/shard_map/upconv_w64/pallas_call | solution.py:597
  155.5 0.0 copy-start.14
  155.5 0.0 copy-start.16
  155.5 0.0 copy-start.22
  155.5 22.8 %conv_w64_256_128.1 = (bf16[130,2,64,128]{3,2,1,0:T(8,128)(2,1)S(1)}, f32[1,128]{1,0:T(1,128)S(1)}) custom-call(bf16[17408,256]{1,0:T(8,128)(2,1)S(1)} %bitcast.55, f32[1,128]{1,0:T(1,128)S(1)} %get-tuple-element.48.refs_1_, f32[2,256]{1,0:T(2,128)S(1)} %copy-done.21, bf16[3,768,128]{2,1,0:T(8,128)(2,1)S(1)} %bitcast.53), custom_call_target="tpu_custom_call" | custom-call | flops 9663676416 | bytes 12582912 | tf_op jit(solution)/shard_map/conv_w64_256_128/pallas_call | solution.py:536
  178.3 0.0 copy-start.23
  178.4 0.0 copy-start.9
  178.4 19.9 %conv_w64_128_128e.1 = (bf16[136,2,64,128]{3,2,1,0:T(8,128)(2,1)S(1)}, f32[1,128]{1,0:T(1,128)S(1)}) custom-call(bf16[16640,128]{1,0:T(8,128)(2,1)S(1)} %bitcast.58, f32[1,128]{1,0:T(1,128)S(1)} %get-tuple-element.50.refs_1_, f32[2,128]{1,0:T(2,128)S(1)} %copy-done.22, bf16[3,384,128]{2,1,0:T(8,128)(2,1)S(1)} %bitcast.54, ...), custom_call_target="tpu_custom_call" | custom-call | flops 4869586944 | bytes 8454144 | tf_op jit(solution)/shard_map/conv_w64_128_128e/pallas_call | solution.py:536
  198.3 12.4 %last_conv.1 = f32[4,96,128]{2,1,0:T(8,128)S(1)} custom-call(bf16[17408,128]{1,0:T(8,128)(2,1)S(1)} %bitcast.32, f32[1,128]{1,0:T(1,128)S(1)} %get-tuple-element.52.tot_ref, f32[2,128]{1,0:T(2,128)S(1)} %copy-done.9, bf16[24,384]{1,0:T(8,128)(2,1)S(1)} %pad_bitcast_fusion.w_ref), custom_call_target="tpu_custom_call" | custom-call | tf_op jit(solution)/shard_map/last_conv/pallas_call | solution.py:669
  210.8 0.4 reshape.126
  211.2 0.4 copy.34
  211.7 0.8 reshape.127
  (44 shorter events, 0.1 us)
Async XLA Ops:
  1.0 64.7 %slice-start = ((s8[4718592]{0:T(1024)(128)(4,1)}), s8[4194304]{0:T(1024)(128)(4,1)S(1)}, s32[]{:S(2)}) async-start(s8[4718592]{0:T(1024)(128)(4,1)} %bitcast.29), calls=%async_computation | async-start | bytes 8388608
  1.0 1.1 copy-start.3
  2.1 1.1 copy-start.5
  3.1 25.4 %copy-start.1 = (bf16[512,1536]{1,0:T(8,128)(2,1)S(1)}, bf16[512,1536]{1,0:T(8,128)(2,1)}, u32[]{:S(2)}) copy-start(bf16[512,1536]{1,0:T(8,128)(2,1)} %wqkv_ref.1) | copy-start | bytes 4718596
  3.1 25.5 %copy-start.2 = (bf16[512,512]{1,0:T(8,128)(2,1)S(1)}, bf16[512,512]{1,0:T(8,128)(2,1)}, u32[]{:S(2)}) copy-start(bf16[512,512]{1,0:T(8,128)(2,1)} %wproj_ref.1) | copy-start | bytes 1572868
  3.1 25.5 %copy-start.4 = (bf16[3,3,16,512]{3,2,1,0:T(8,128)(2,1)S(1)}, bf16[3,3,16,512]{3,2,1,0:T(8,128)(2,1)}, u32[]{:S(2)}) copy-start(bf16[3,3,16,512]{3,2,1,0:T(8,128)(2,1)} %param.39) | copy-start | bytes 442372
  3.1 25.5 %copy-start.6 = (f32[2,512]{1,0:T(2,128)S(1)}, f32[2,512]{1,0:T(2,128)}, u32[]{:S(2)}) copy-start(f32[2,512]{1,0:T(2,128)} %norm_ref.2) | copy-start | bytes 12292
  3.1 54.0 %copy-start = (bf16[3,3,512,512]{3,2,1,0:T(8,128)(2,1)S(1)}, bf16[3,3,512,512]{3,2,1,0:T(8,128)(2,1)}, u32[]{:S(2)}) copy-start(bf16[3,3,512,512]{3,2,1,0:T(8,128)(2,1)} %param.44) | copy-start | bytes 14155780
  3.2 54.0 %copy-start.8 = (f32[2,512]{1,0:T(2,128)S(1)}, f32[2,512]{1,0:T(2,128)}, u32[]{:S(2)}) copy-start(f32[2,512]{1,0:T(2,128)} %refs_2_.8) | copy-start | bytes 12292
  3.2 62.5 %slice-start.1 = ((s8[4718592]{0:T(1024)(128)(4,1)}), s8[524288]{0:T(1024)(128)(4,1)S(1)}, s32[]{:S(2)}) async-start(s8[4718592]{0:T(1024)(128)(4,1)} %bitcast.29), calls=%async_computation.1 | async-start | bytes 1048576
  28.6 37.1 %copy-start.7 = (f32[2,512]{1,0:T(2,128)S(1)}, f32[2,512]{1,0:T(2,128)}, u32[]{:S(2)}) copy-start(f32[2,512]{1,0:T(2,128)} %refs_2_.9) | copy-start | bytes 12292
  28.6 39.3 %slice-start.2 = ((s8[4718592]{0:T(1024)(128)(4,1)}), s8[4194304]{0:T(1024)(128)(4,1)S(1)}, s32[]{:S(2)}) async-start(s8[4718592]{0:T(1024)(128)(4,1)} %bitcast.38), calls=%async_computation.2 | async-start | bytes 8388608
  57.2 10.7 %slice-start.3 = ((s8[4718592]{0:T(1024)(128)(4,1)}), s8[524288]{0:T(1024)(128)(4,1)S(1)}, s32[]{:S(2)}) async-start(s8[4718592]{0:T(1024)(128)(4,1)} %bitcast.38), calls=%async_computation.3 | async-start | bytes 1048576
  57.2 19.5 %slice-start.4 = ((s8[4718592]{0:T(1024)(128)(4,1)}), s8[4194304]{0:T(1024)(128)(4,1)S(1)}, s32[]{:S(2)}) async-start(s8[4718592]{0:T(1024)(128)(4,1)} %bitcast.41), calls=%async_computation.4 | async-start | bytes 8388608
  65.7 11.0 %slice-start.5 = ((s8[4718592]{0:T(1024)(128)(4,1)}), s8[524288]{0:T(1024)(128)(4,1)S(1)}, s32[]{:S(2)}) async-start(s8[4718592]{0:T(1024)(128)(4,1)} %bitcast.41), calls=%async_computation.5 | async-start | bytes 1048576
  67.9 8.9 %copy-start.17 = (f32[2,512]{1,0:T(2,128)S(1)}, f32[2,512]{1,0:T(2,128)}, u32[]{:S(2)}) copy-start(f32[2,512]{1,0:T(2,128)} %refs_2_.10) | copy-start | bytes 12292
  67.9 21.0 %slice-start.6 = ((s8[4718592]{0:T(1024)(128)(4,1)}), s8[4194304]{0:T(1024)(128)(4,1)S(1)}, s32[]{:S(2)}) async-start(s8[4718592]{0:T(1024)(128)(4,1)} %bitcast.44), calls=%async_computation.6 | async-start | bytes 8388608
  76.8 12.1 %slice-start.7 = ((s8[4718592]{0:T(1024)(128)(4,1)}), s8[524288]{0:T(1024)(128)(4,1)S(1)}, s32[]{:S(2)}) async-start(s8[4718592]{0:T(1024)(128)(4,1)} %bitcast.44), calls=%async_computation.7 | async-start | bytes 1048576
  76.8 12.1 %copy-start.18 = (f32[2,512]{1,0:T(2,128)S(1)}, f32[2,512]{1,0:T(2,128)}, u32[]{:S(2)}) copy-start(f32[2,512]{1,0:T(2,128)} %refs_2_.11) | copy-start | bytes 12292
  76.8 18.9 %slice-start.8 = ((s8[4718592]{0:T(1024)(128)(4,1)}), s8[4194304]{0:T(1024)(128)(4,1)S(1)}, s32[]{:S(2)}) async-start(s8[4718592]{0:T(1024)(128)(4,1)} %bitcast.47), calls=%async_computation.8 | async-start | bytes 8388608
  88.9 6.8 %slice-start.9 = ((s8[4718592]{0:T(1024)(128)(4,1)}), s8[524288]{0:T(1024)(128)(4,1)S(1)}, s32[]{:S(2)}) async-start(s8[4718592]{0:T(1024)(128)(4,1)} %bitcast.47), calls=%async_computation.9 | async-start | bytes 1048576
  95.7 15.7 %copy-start.10 = (bf16[3,3,512,256]{3,2,1,0:T(8,128)(2,1)S(1)}, bf16[3,3,512,256]{3,2,1,0:T(8,128)(2,1)}, u32[]{:S(2)}) copy-start(bf16[3,3,512,256]{3,2,1,0:T(8,128)(2,1)} %param.54) | copy-start | bytes 7077892
  95.8 15.7 %copy-start.19 = (f32[2,512]{1,0:T(2,128)S(1)}, f32[2,512]{1,0:T(2,128)}, u32[]{:S(2)}) copy-start(f32[2,512]{1,0:T(2,128)} %refs_2_.12) | copy-start | bytes 12292
  111.4 18.1 %copy-start.11 = (bf16[3,3,256,256]{3,2,1,0:T(8,128)(2,1)S(1)}, bf16[3,3,256,256]{3,2,1,0:T(8,128)(2,1)}, u32[]{:S(2)}) copy-start(bf16[3,3,256,256]{3,2,1,0:T(8,128)(2,1)} %param.56) | copy-start | bytes 3538948
  111.4 18.1 %copy-start.15 = (bf16[512,256]{1,0:T(8,128)(2,1)S(1)}, bf16[512,256]{1,0:T(8,128)(2,1)}, u32[]{:S(2)}) copy-start(bf16[512,256]{1,0:T(8,128)(2,1)} %refs_5_.2) | copy-start | bytes 786436
  111.5 18.1 %copy-start.20 = (f32[2,256]{1,0:T(2,128)S(1)}, f32[2,256]{1,0:T(2,128)}, u32[]{:S(2)}) copy-start(f32[2,256]{1,0:T(2,128)} %refs_2_.13) | copy-start | bytes 6148
  129.6 8.2 %copy-start.12 = (bf16[3,3,256,256]{3,2,1,0:T(8,128)(2,1)S(1)}, bf16[3,3,256,256]{3,2,1,0:T(8,128)(2,1)}, u32[]{:S(2)}) copy-start(bf16[3,3,256,256]{3,2,1,0:T(8,128)(2,1)} %param.58) | copy-start | bytes 3538948
  137.8 17.6 %copy-start.13 = (bf16[3,3,256,128]{3,2,1,0:T(8,128)(2,1)S(1)}, bf16[3,3,256,128]{3,2,1,0:T(8,128)(2,1)}, u32[]{:S(2)}) copy-start(bf16[3,3,256,128]{3,2,1,0:T(8,128)(2,1)} %param.60) | copy-start | bytes 1769476
  137.8 17.6 %copy-start.21 = (f32[2,256]{1,0:T(2,128)S(1)}, f32[2,256]{1,0:T(2,128)}, u32[]{:S(2)}) copy-start(f32[2,256]{1,0:T(2,128)} %refs_2_.14) | copy-start | bytes 6148
  155.5 22.9 %copy-start.14 = (bf16[3,3,128,128]{3,2,1,0:T(8,128)(2,1)S(1)}, bf16[3,3,128,128]{3,2,1,0:T(8,128)(2,1)}, u32[]{:S(2)}) copy-start(bf16[3,3,128,128]{3,2,1,0:T(8,128)(2,1)} %param.62) | copy-start | bytes 884740
  155.5 22.9 %copy-start.16 = (bf16[256,128]{1,0:T(8,128)(2,1)S(1)}, bf16[256,128]{1,0:T(8,128)(2,1)}, u32[]{:S(2)}) copy-start(bf16[256,128]{1,0:T(8,128)(2,1)} %refs_5_.3) | copy-start | bytes 196612
  155.5 22.9 %copy-start.22 = (f32[2,128]{1,0:T(2,128)S(1)}, f32[2,128]{1,0:T(2,128)}, u32[]{:S(2)}) copy-start(f32[2,128]{1,0:T(2,128)} %refs_2_.15) | copy-start | bytes 3076
  178.3 20.0 %copy-start.23 = (bf16[3,3,128,3]{2,3,1,0:T(4,128)(2,1)S(1)}, bf16[3,3,128,3]{2,3,1,0:T(4,128)(2,1)}, u32[]{:S(2)}) copy-start(bf16[3,3,128,3]{2,3,1,0:T(4,128)(2,1)} %param.65) | copy-start | bytes 20740
  178.4 20.0 %copy-start.9 = (f32[2,128]{1,0:T(2,128)S(1)}, f32[2,128]{1,0:T(2,128)}, u32[]{:S(2)}) copy-start(f32[2,128]{1,0:T(2,128)} %norm_ref.3) | copy-start | bytes 3076
where the time goes:
time: 213 us; the launch traced here: 212 us
  Pallas kernels  207 us (97%)
  local copies, waits for them, and re-layouts  5 us (2%)
    pallas_call x8, Pallas kernels, conv(): pl.pallas_call(functools.partial(conv_kernel, cfg), out_shape=outs, in_sp...  98.5 us
    pallas_call x3, Pallas kernels, upconv(): pl.pallas_call(functools.partial(upconv_kernel, (net_shape, half, hs, blk...  42 us
    pallas_call x1, Pallas kernels, attention(): pl.pallas_call(functools.partial(attention_kernel, net_shape), out_shape=...  28.5 us
    pallas_call x1, Pallas kernels, mlp(): pl.pallas_call(functools.partial(mlp_kernel, net_shape), out_shape=jax.Sh...  25.4 us
    pallas_call x1, Pallas kernels, last_conv(): pl.pallas_call(functools.partial(last_kernel, (net_shape, wid, h, blk, oc...  12.4 us

commit v1 on v0

--- a/solution.py
+++ b/solution.py
@@ -9,6 +9,7 @@
 GROUPS = 32
 LOG2_E = 1.4426950408889634
 LANES = 128
+SUB = 8
 BASE = 16
 F32, BF16 = jnp.float32, jnp.bfloat16
 MESH = pl.DeviceIdType.MESH
@@ -34,6 +35,10 @@
         ref[...] = jnp.zeros_like(ref)
 
 
+def repeat(count, step):
+    lax.fori_loop(0, count, step, 0)
+
+
 def iota(shape, dim):
     return lax.broadcasted_iota(jnp.int32, shape, dim)
 
@@ -61,15 +66,16 @@
 
     def for_others(self, act, row_step=1):
         cols = [lax.rem(self.col + k, self.n_col) for k in range(self.n_col)]
-        for col in cols[1:]:
-            act({'row': self.row, 'col': col})
+        n_row = self.n_row // row_step
 
         def step(k, carry):
-            row = lax.rem(self.row + k * row_step, self.n_row)
+            row = lax.rem(self.row + (1 + lax.rem(k + n_row // 2 - 1, n_row - 1)) * row_step, self.n_row)
             for col in cols:
                 act({'row': row, 'col': col})
             return carry
-        lax.fori_loop(1, self.n_row // row_step, step, 0)
+        repeat(n_row - 1, step)
+        for col in cols[1:]:
+            act({'row': self.row, 'col': col})
         return self.n // row_step - 1
 
     def beside(self, ahead):
@@ -108,7 +114,7 @@
     return scratch
 
 
-def exchange(net, stat, stat_ref, recv, sems, tot_ref, sides=None):
+def exchange(net, stat, stat_ref, recv, sems, tot_ref, sides=None, meanwhile=None):
     stat_ref[...] = stat
     net.all_here()
     wait = net.to_others(stat_ref, recv, sems)
@@ -120,6 +126,8 @@
     for copy, _, _ in side_copies:
         copy.start()
     recv[net.strip] = stat
+    if meanwhile:
+        meanwhile()
     wait()
     tot_ref[...] = jnp.sum(recv[...], axis=0)
     for copy, dst, side in side_copies:
@@ -128,7 +136,7 @@
 
 
 def sum_scratch(ch):
-    return [pltpu.VMEM((8, ch), F32)] * 2
+    return [pltpu.VMEM((SUB, ch), F32)] * 2
 
 
 def comm_params(cid, mib):
@@ -136,39 +144,45 @@
 
 
 def mlp_kernel(net_shape, x_ref, mod_ref, w1_ref, w2_ref, wf_ref, o_ref,
-               w1_buf, w2_buf, act_ref, acc_ref, tok_ref, mix_ref, recv, w_sems, sems, pass_sems):
+               w1_buf, w2_buf, act_ref, acc_ref, part_ref, tok_ref, mix_ref, recv, w_sems, sems, swap_sems, pass_sems):
     net = Net(*net_shape)
     n_buf, blk = w1_buf.shape[0], w1_buf.shape[2]
-    n_cut = w1_ref.shape[1] // blk
+    n_cut = w1_ref.shape[1] // blk // 2
+    core = lax.rem(net.row, 2)
+    partner = {'row': net.row + 1 - 2 * core, 'col': net.col}
+    n_tok = x_ref.shape[0]
 
     def loads(i):
-        part, slot = aligned(i * blk, blk, blk), lax.rem(i, n_buf)
+        part, slot = aligned((core * n_cut + i) * blk, blk, blk), lax.rem(i, n_buf)
         return [pltpu.make_async_copy(w1_ref.at[:, part], w1_buf.at[slot], w_sems.at[0, slot]),
                 pltpu.make_async_copy(w2_ref.at[part], w2_buf.at[slot], w_sems.at[1, slot])]
-    for i in range(n_buf - 1):
+    for i in range(n_cut):
         for load in loads(i):
             load.start()
     net.greet()
     shift1, scale1, gate1, shift2, scale2 = [mod_ref[pl.ds(i, 1)] for i in range(5)]
     x = x_ref[...].astype(F32)
     act = (layer_norm(x) * (1.0 + scale1) + shift1).astype(BF16)
-    act_ref[...] = act
+    act_ref[0] = act
     clear(acc_ref)
+    net.all_here()
+    swap = send(act_ref.at[0], act_ref.at[1], swap_sems.at[0], partner)
+    swap.start()
+    swap.wait()
 
     def step(i, carry):
-        @pl.when(i + n_buf - 1 < n_cut)
-        def _():
-            for load in loads(i + n_buf - 1):
-                load.start()
         load1, load2 = loads(i)
         slot = lax.rem(i, n_buf)
         load1.wait()
-        hid = jax.nn.gelu(dot(act_ref[...], w1_buf[slot]), approximate=True).astype(BF16)
+        hid = jax.nn.gelu(dot(act_ref[...].reshape(2 * n_tok, -1), w1_buf[slot]), approximate=True).astype(BF16)
         load2.wait()
-        acc_ref[...] += dot(hid, w2_buf[slot])
+        acc_ref[...] += dot(hid, w2_buf[slot]).reshape(acc_ref.shape)
         return carry
-    lax.fori_loop(0, n_cut, step, 0)
-    acc = acc_ref[...]
+    repeat(n_cut, step)
+    swap = send(acc_ref.at[1], part_ref, swap_sems.at[1], partner)
+    swap.start()
+    swap.wait()
+    acc = acc_ref[0] + part_ref[...]
     y = (x + gate1 * acc).astype(BF16)
     fin = (layer_norm(y.astype(F32)) * (1.0 + scale2) + shift2).astype(BF16)
     tok_ref[...] = dot_t(fin, wf_ref[...])
@@ -178,13 +192,11 @@
     for p in range(2):
         mix_ref[pl.ds(p, rows, stride=2), :] = jnp.concatenate([t[:, p * part:(p + 1) * part] for t in toks], axis=1)
     recv[net.strip] = mix_ref[...].astype(BF16)
-    net.all_here()
     net.to_others(recv.at[net.strip], recv, sems, 2)()
-    core = lax.rem(net.row, 2)
     copies = []
     for i in range(net.n_row // 2):
         line = recv.at[pl.ds((2 * i + core) * net.n_col, net.n_col)]
-        copies.append(send(line, line, pass_sems.at[i], {'row': net.row + 1 - 2 * core, 'col': net.col}))
+        copies.append(send(line, line, pass_sems.at[i], partner))
         copies[-1].start()
     for copy in copies:
         copy.wait()
@@ -195,7 +207,8 @@
     n = net_shape[0] * net_shape[1]
     n_tok, d = x.shape
     hid, patch = w_fc1.shape[1], w_final.shape[1]
-    n_buf, blk = 4, 768
+    n_buf = 4
+    blk = hid // (2 * n_buf)
     rows = 2 * n_tok // tok_w
     lat = (rows, n_tok * patch // rows)
     hbm = pl.BlockSpec(memory_space=pltpu.HBM)
@@ -205,9 +218,9 @@
         in_specs=[VMEM_SPEC, VMEM_SPEC, hbm, hbm, VMEM_SPEC],
         out_specs=VMEM_SPEC,
         scratch_shapes=[pltpu.VMEM((n_buf, d, blk), BF16), pltpu.VMEM((n_buf, blk, d), BF16),
-                        pltpu.VMEM(x.shape, BF16), pltpu.VMEM(x.shape, F32),
+                        pltpu.VMEM((2,) + x.shape, BF16), pltpu.VMEM((2,) + x.shape, F32), pltpu.VMEM(x.shape, F32),
                         pltpu.VMEM((n_tok, patch), F32), pltpu.VMEM(lat, F32), pltpu.VMEM((n,) + lat, BF16),
-                        pltpu.SemaphoreType.DMA((2, n_buf)), PAIR_SEM, pltpu.SemaphoreType.DMA((net_shape[0] // 2, 2))],
+                        pltpu.SemaphoreType.DMA((2, n_buf)), PAIR_SEM, pltpu.SemaphoreType.DMA((2, 2)), pltpu.SemaphoreType.DMA((net_shape[0] // 2, 2))],
         compiler_params=comm_params(cid, 48),
         name='mlp',
     )(x, mod_vec, w_fc1, w_fc2, w_final.T)
@@ -226,7 +239,7 @@
 
 
 def norm_coefs(tot, norm_ref, ch, count):
-    avg = jnp.broadcast_to(tot / count, (8, LANES))
+    avg = jnp.broadcast_to(tot / count, (SUB, LANES))
     shape = (LANES, ch)
     mean, square = [exact_dot(avg, in_group(iota(shape, 1), iota(shape, 0) - at, ch // GROUPS)) for at in (0, GROUPS)]
     scale = lax.rsqrt(square - jnp.square(mean) + 1e-6) * norm_ref[0:1]
@@ -234,7 +247,7 @@
 
 
 def fold8(v):
-    return jnp.sum(v.reshape(v.shape[0] // 8, 8, v.shape[1]), axis=0)
+    return jnp.sum(v.reshape(v.shape[0] // SUB, SUB, v.shape[1]), axis=0)
 
 
 def attention_kernel(net_shape, lat_ref, win_ref, norm_ref, wqkv_ref, wproj_ref, out_ref, tot_ref,
@@ -257,7 +270,7 @@
             if 0 <= src < wid:
                 toe_ref[x, pl.ds(tap // 3 * LANES + src * lat_c, lat_c), :] = win_ref[tap]
     clear(s1_ref, s2_ref)
-    blk = 256
+    blk = 1024
     per_col = rows // blk
 
     def conv_step(i, carry):
@@ -267,7 +280,7 @@
         s1_ref[...] += fold8(yf)
         s2_ref[...] += fold8(yf * yf)
         return carry
-    lax.fori_loop(0, wid * per_col, conv_step, 0)
+    repeat(wid * per_col, conv_step)
     mean, scale, shift = norm_coefs(group_sums(s1_ref[...], s2_ref[...]), norm_ref, ch, float(rows * wid * (ch // GROUPS)))
 
     for x in range(wid):
@@ -286,7 +299,7 @@
             m = jnp.maximum(m, s[:, j * LANES:(j + 1) * LANES])
         m_ref[...] = m
         return carry
-    lax.fori_loop(0, nk, score_step, 0)
+    repeat(nk, score_step)
     m_ref[...] = jnp.broadcast_to(jnp.max(m_ref[...], axis=1, keepdims=True), m_ref.shape)
     clear(l_ref, acc_ref)
 
@@ -301,7 +314,7 @@
         l_ref[...] = tot_l
         acc_ref[...] += dot(jnp.concatenate(parts, axis=1), fmap_ref[aligned(i * kb, kb, kb), :])
         return carry
-    lax.fori_loop(0, nk, value_step, 0)
+    repeat(nk, value_step)
     pn = acc_ref[...] / jnp.sum(l_ref[...], axis=1, keepdims=True)
     pn = ((pn - mean) * scale + shift).astype(BF16)
     att = dot(pn, wqkv_ref[:, 2 * ch:]).astype(BF16)
@@ -321,7 +334,7 @@
     wid = lat.shape[1] // lat_c
     own = rows // n
     n_q = own * wid
-    kb = 512
+    kb = 2048
     return pl.pallas_call(
         functools.partial(attention_kernel, net_shape),
         out_shape=[jax.ShapeDtypeStruct((own + 2, wid, ch), BF16), TOTALS],
@@ -343,8 +356,8 @@
         even, odd = jnp.split(y.reshape(n_px // wid, 2, wid // 2, ch), 2, axis=1)
         far = shifted((odd if by == 1 else even).reshape(n_px // 2, ch), wid // 2, by).reshape(even.shape)
         return jnp.concatenate([far, even] if by == 1 else [odd, far], axis=1).reshape(n_px, ch)
-    tiles = pltpu.roll(y, by % n_px, 0).reshape(n_px // wid, wid // 8, 8, ch)
-    at, sub = (0, 0) if by > 0 else (wid // 8 - 1, 7)
+    tiles = pltpu.roll(y, by % n_px, 0).reshape(n_px // wid, wid // SUB, SUB, ch)
+    at, sub = (0, 0) if by > 0 else (wid // SUB - 1, 7)
     edge = tiles[:, at:at + 1]
     edge = jnp.where(iota(edge.shape, 2) == sub, 0.0, edge)
     parts = [tiles[:, :at], edge, tiles[:, at + 1:]]
@@ -373,7 +386,7 @@
             row = b * blk + j
             if self.n_out > blk:
                 row = jnp.minimum(row, self.n_out + 1)
-            v = self.x_ref[aligned(row * wid, together * wid, 8), :].astype(F32)
+            v = self.x_ref[aligned(row * wid, together * wid, SUB), :].astype(F32)
             if together == 1:
                 keep = jnp.where(self.inside(row), 1.0, 0.0)
                 y = silu_of_half(v * (scale * keep) + shift * keep)
@@ -404,14 +417,13 @@
         return pltpu.VMEM(shape, F32 if self.wid < 16 else BF16)
 
     def product(self, buf, w_ref):
+        m = self.blk * self.wid // (2 if self.pair else 1)
+        if self.pair:
+            lhs = jnp.concatenate([buf[t % 2, t // 2 * self.wid:t // 2 * self.wid + m, :] for t in range(4)], axis=1)
+            return dot(lhs, w_ref[...])
         acc = None
-        m = self.blk * self.wid // (2 if self.pair else 1)
-        for t in range(4 if self.pair else 3):
-            if self.pair:
-                lhs = buf[t % 2, t // 2 * self.wid:t // 2 * self.wid + m, :]
-            else:
-                lhs = buf[t * self.wid:t * self.wid + m, :].astype(BF16)
-            part = dot(lhs, w_ref[t])
+        for t in range(3):
+            part = dot(buf[t * self.wid:t * self.wid + m, :].astype(BF16), w_ref[t])
             acc = part if acc is None else acc + part
         return acc
 
@@ -425,7 +437,7 @@
                 self.fill(bufs[0], 2 * i + 2, bufs[1])
                 work(bufs[1], 2 * i + 1)
                 return carry
-            lax.fori_loop(0, n_blk // 2, step, 0)
+            repeat(n_blk // 2, step)
         if n_blk % 2:
             work(bufs[0], n_blk - 1)
 
@@ -433,19 +445,21 @@
 def paired_weights(w_ref, wp_ref):
     oc = w_ref.shape[2]
     clear(wp_ref)
+    k = w_ref.shape[1]
     for t in range(3):
-        wp_ref[t, :, :oc] = w_ref[t]
-        wp_ref[t + 1, :, oc:] = w_ref[t]
+        wp_ref[t * k:(t + 1) * k, :oc] = w_ref[t]
+        wp_ref[(t + 1) * k:(t + 2) * k, oc:] = w_ref[t]
 
 
 def conv_kernel(cfg, *refs):
-    net_shape, wid, h, blk, out_ext, pair, shortcut, stats, edge = cfg
+    net_shape, wid, h, blk, out_ext, pair, shortcut, stats, edge, skip_blk = cfg
     refs = iter(refs)
     x_ref, norm_tot_ref, norm_ref, w_ref = [next(refs) for _ in 'abcd']
     short_ref = next(refs) if shortcut else None
-    skip_ref = next(refs) if shortcut == 'matmul' else None
+    skip_ref = next(refs) if skip_blk else None
     out_ref = next(refs)
     tot_ref = next(refs) if stats else None
+    skip_out_ref = next(refs) if skip_blk else None
     buf0, buf1, s1_ref, s2_ref = [next(refs) for _ in 'abcd']
     wp_ref = next(refs) if pair else w_ref
     net_refs = list(refs)
@@ -481,19 +495,16 @@
                 val = acc[:, a * oc:(a + 1) * oc]
                 here = pl.ds(edge // 2 + k0 // 2, blk // 2)
                 if shortcut:
-                    src = short_ref[pl.ds(k0 // 2, blk // 2), a]
-                    val = dot(src.reshape(blk // 2 * wid, src.shape[-1]), skip_ref[...]) + val
+                    val = short_ref[pl.ds(k0 // 2, blk // 2), a].reshape(val.shape) + val
                 y = val.astype(BF16)
                 out_ref[here, a] = y.reshape(blk // 2, wid, oc)
                 if stats:
                     count(y, k0 + a, 2)
         else:
-            if shortcut == 'add':
-                acc = short_ref[aligned(k0 * wid, blk * wid, 8), :].astype(F32) + acc
-            elif shortcut == 'matmul':
-                acc = dot(short_ref[aligned(k0 * wid, blk * wid, 8), :], skip_ref[...]) + acc
+            if shortcut:
+                acc = short_ref[aligned(k0 * wid, blk * wid, SUB), :].astype(F32) + acc
             y = acc.astype(BF16)
-            out_ref[aligned((k0 + edge) * wid, blk * wid, 8), :] = y
+            out_ref[aligned((k0 + edge) * wid, blk * wid, SUB), :] = y
             if stats:
                 count(y, k0, 1)
     rows.run((buf0, buf1), work)
@@ -510,26 +521,36 @@
             def part(row):
                 return out_ref.at[row // 2] if pair else out_ref.at[pl.ds(row * wid, edge * wid)]
             sides = (part(edge), part(h), part(0), part(h + edge), *net_refs[3:])
-        exchange(net, group_sums(s1_ref[...], s2_ref[...]), *net_refs[:3], tot_ref, sides)
-
-
-def conv(x, tot, norm, w, h, wid, net_shape, blk, out_ext, stats, edge, pair, cid, *shortcut):
+
+        def skip_step(b, carry):
+            here = aligned(b * skip_blk * wid, skip_blk * wid, SUB)
+            skip_out_ref[here, :] = dot(x_ref[here, :], skip_ref[...])
+            return carry
+
+        def skip_all():
+            repeat(skip_out_ref.shape[0] // (skip_blk * wid), skip_step)
+        exchange(net, group_sums(s1_ref[...], s2_ref[...]), *net_refs[:3], tot_ref, sides, skip_all if skip_blk else None)
+
+
+def conv(x, tot, norm, w, h, wid, net_shape, blk, out_ext, stats, edge, pair, cid, short, skip):
     n = net_shape[0] * net_shape[1]
     ch, oc = w.shape[2:]
     args = [x, tot, norm, w.reshape(3, 3 * ch, oc)]
-    for short in shortcut[:1]:
-        args.append(short.reshape(-1, 2, wid, short.shape[-1]) if pair else short)
-    args += shortcut[1:]
+    for src in short:
+        args.append(src.reshape(-1, 2, wid, src.shape[-1]) if pair else src)
+    args += skip[:1]
     n_out = h + 2 * out_ext
     rows = -(-n_out // blk) * blk + 2 * edge
     outs = [jax.ShapeDtypeStruct((rows // 2, 2, wid, oc) if pair else (rows * wid, oc), BF16)]
     if stats:
         outs.append(TOTALS)
-    cfg = (net_shape, wid, h, blk, out_ext, pair, ('', 'add', 'matmul')[len(shortcut)], stats, edge)
+    cfg = (net_shape, wid, h, blk, out_ext, pair, bool(short), stats, edge, skip[1] if skip else 0)
+    if skip:
+        outs.append(jax.ShapeDtypeStruct((skip[2] * wid, skip[0].shape[1]), F32))
     layout = Rows(None, x, None, wid, h, None, n_out, blk, pair)
     scratch = [layout.buffer(), layout.buffer(), *sum_scratch(oc)]
     if pair:
-        scratch.append(pltpu.VMEM((4, 3 * ch, 2 * oc), BF16))
+        scratch.append(pltpu.VMEM((12 * ch, 2 * oc), BF16))
     if stats:
         scratch += net_scratch(n, ((2, wid, oc) if pair else (edge * wid, oc)) if edge else None)
     px = n_out * wid
@@ -556,7 +577,7 @@
 
     def step(b, carry):
         k0 = jnp.minimum(b * blk, n_k - blk) if n_k > blk else 0
-        x = x_ref[aligned(k0 * half, more, 8), :]
+        x = x_ref[aligned(k0 * half, more, SUB), :]
         rows = []
         for dx in range(3):
             above, mid, below = [dot(x, w_ref[3 * dy + dx]) for dy in range(3)]
@@ -585,7 +606,7 @@
     if n_k == blk:
         step(0, 0)
     else:
-        lax.fori_loop(0, -(-n_k // blk), step, 0)
+        repeat(-(-n_k // blk), step)
     exchange(net, group_sums(s1_ref[...], s2_ref[...]), stat_ref, recv, sems, tot_ref)
 
 
@@ -599,7 +620,7 @@
         out_shape=[jax.ShapeDtypeStruct((n_k, 2, 2 * half, oc), BF16), TOTALS],
         in_specs=[VMEM_SPEC] * 2, out_specs=[VMEM_SPEC] * 2,
         scratch_shapes=[*sum_scratch(oc),
-                        pltpu.VMEM((2, oc // LANES, 2 * blk * half if half < BASE else 8, LANES), F32)] + net_scratch(n),
+                        pltpu.VMEM((2, oc // LANES, 2 * blk * half if half < BASE else SUB, LANES), F32)] + net_scratch(n),
         compiler_params=comm_params(cid, 28),
         cost_estimate=pl.CostEstimate(flops=5 * ch * oc * px, bytes_accessed=2 * px * (ch + oc), transcendentals=0),
         name='upconv_w%d' % (2 * half),
@@ -636,7 +657,7 @@
     def work(buf, b):
         for q in range(net.n_col):
             z = dot_t(w_ref[...], buf[q])
-            z = z[:8, :m] + z[8:16, tile:tile + m] + z[16:, 2 * tile:2 * tile + m]
+            z = z[:SUB, :m] + z[SUB:16, tile:tile + m] + z[16:, 2 * tile:2 * tile + m]
             for c in range(oc):
                 for t in range(m // LANES):
                     mine[q, pl.ds(c * per + b * (m // LANES) + t, 1), :] = z[c:c + 1, t * LANES:(t + 1) * LANES]
@@ -663,7 +684,7 @@
 def last_conv(x, tot, norm, w, h, wid, net_shape, blk, cid):
     n_col = net_shape[1]
     ch, oc = w.shape[2:]
-    wt = jnp.zeros((3, 8, 3 * ch), BF16).at[:, :oc].set(w.reshape(3, 3 * ch, oc).transpose(0, 2, 1))
+    wt = jnp.zeros((3, SUB, 3 * ch), BF16).at[:, :oc].set(w.reshape(3, 3 * ch, oc).transpose(0, 2, 1))
     buf = pltpu.VMEM((n_col, (blk + 2) * wid // n_col, 3 * ch), BF16)
     shape = (n_col, oc * h * wid // n_col // LANES, LANES)
     return pl.pallas_call(
@@ -688,13 +709,14 @@
     u = f.reshape(-1, f.shape[-1])
     blocks = [(norm0_a, conv0_a, norm0_b, conv0_b, (), upconv_0, h, h + 2, h + 1),
               (norm1_a, conv1_a, norm1_b, conv1_b, (), upconv_1, 16, 11, 13),
-              (norm2_a, conv2_a, norm2_b, conv2_b, (skip_2,), upconv_2, 8, 10, 10),
-              (norm3_a, conv3_a, norm3_b, conv3_b, (skip_3,), None, 8, 16, 0)]
+              (norm2_a, conv2_a, norm2_b, conv2_b, (skip_2,), upconv_2, 16, 10, 10),
+              (norm3_a, conv3_a, norm3_b, conv3_b, (skip_3,), None, 16, 16, 0)]
     cid = 3
     for norm_a, conv_a, norm_b, conv_b, skip, up, blk_a, blk_b, blk_up in blocks:
         last = up is None
-        g, tot = conv(u, tot, norm_a, conv_a, h, wid, net_shape, blk_a, 0, True, 2, last, cid)
-        f, *tot = conv(g, tot, norm_b, conv_b, h, wid, net_shape, blk_b, 1, last, 0, last, cid + 1, u, *skip)
+        skip = [(m, blk_b, -(-(h + 2) // blk_b) * blk_b) for m in skip]
+        g, tot, *short = conv(u, tot, norm_a, conv_a, h, wid, net_shape, blk_a, 0, True, 2, last, cid, (), *skip or [()])
+        f, *tot = conv(g, tot, norm_b, conv_b, h, wid, net_shape, blk_b, 1, last, 0, last, cid + 1, short or (u,), ())
         if not last:
             u, tot = upconv(f, up, h, wid, net_shape, blk_up, cid + 2)
             h, wid = 2 * h, 2 * wid

time: 213 us -> 196 us (0.920)
  Pallas kernels: 207 us -> 190 us
    pallas_call x1, Pallas kernels: 28.5 us -> 21.3 us  [attention(): pl.pallas_call(functools.partial(attention_kernel, net_shape), out_shape=...]
    pallas_call x8, Pallas kernels: 98.5 us -> 93.5 us  [conv(): pl.pallas_call(functools.partial(conv_kernel, cfg), out_shape=outs, in_sp...]
    pallas_call x1, Pallas kernels: 25.4 us -> 22.3 us  [mlp(): pl.pallas_call(functools.partial(mlp_kernel, net_shape), out_shape=jax.Sh...]
where the time goes in v1:
time: 196 us
  Pallas kernels  190 us (97%)
  local copies, waits for them, and re-layouts  5 us (3%)
    pallas_call x8, Pallas kernels, conv(): pl.pallas_call(functools.partial(conv_kernel, cfg), out_shape=outs, in_sp...  93.5 us
    pallas_call x3, Pallas kernels, upconv(): pl.pallas_call(functools.partial(upconv_kernel, (net_shape, half, hs, blk...  40.8 us
    pallas_call x1, Pallas kernels, mlp(): pl.pallas_call(functools.partial(mlp_kernel, net_shape), out_shape=jax.Sh...  22.3 us
    pallas_call x1, Pallas kernels, attention(): pl.pallas_call(functools.partial(attention_kernel, net_shape), out_shape=...  21.3 us
    pallas_call x1, Pallas kernels, last_conv(): pl.pallas_call(functools.partial(last_kernel, (net_shape, wid, h, blk, oc...  12.5 us

profile of v1, /device:TPU:97, one launch (start us, length us, event | category | flops | bytes accessed | tf_op | source)
XLA Modules:
  0.0 196.0 jit_solution(8490702504057226001)
XLA Ops:
  0.0 1.0 reshape.107.x_ref
  1.0 0.0 slice-start
  1.0 0.0 copy-start.3
  1.0 1.1 copy-done.3
  2.1 1.1 copy-done.5
  3.1 0.0 copy-start
  3.2 0.0 copy-start.8
  3.2 22.3 %mlp.1 = bf16[32,32,128]{2,1,0:T(8,128)(2,1)S(1)} custom-call(bf16[64,1536]{1,0:T(8,128)(2,1)S(1)} %reshape.107.x_ref, f32[5,1536]{1,0:T(8,128)S(1)} %copy-done.5, bf16[1536,6144]{1,0:T(8,128)(2,1)} %w1_ref.1, bf16[6144,1536]{1,0:T(8,128)(2,1)} %w2_ref.1, bf16[64,1536]{1,0:T(8,128)(2,1)S(1)} %bitcast.37), custom_call_target="tpu_custom_call" | custom-call | tf_op jit(solution)/shard_map/mlp/pallas_call | solution.py:215
  25.5 0.0 copy-start.7
  25.5 0.0 slice-start.2
  25.5 21.3 %attention.1 = (bf16[34,8,512]{2,1,0:T(8,128)(2,1)S(1)}, f32[1,128]{1,0:T(1,128)S(1)}) custom-call(bf16[1024,128]{1,0:T(8,128)(2,1)S(1)} %bitcast.36, bf16[9,16,512]{2,1,0:T(8,128)(2,1)S(1)} %bitcast.38, f32[2,512]{1,0:T(2,128)S(1)} %copy-done.6, bf16[512,1536]{1,0:T(8,128)(2,1)S(1)} %copy-done.1, bf16[512,512]{1,0:T(8,128)(2,1)S(1)} %copy-done.2), custom_call_target="tpu_custom_call" | custom-call | tf_op jit(solution)/shard_map/attention/pallas_call | solution.py:338
  46.9 0.0 slice-start.3
  46.9 0.0 slice-start.4
  46.9 7.7 %conv_w8_512_512.1 = (bf16[288,512]{1,0:T(8,128)(2,1)S(1)}, f32[1,128]{1,0:T(1,128)S(1)}) custom-call(bf16[272,512]{1,0:T(8,128)(2,1)S(1)} %bitcast.34, f32[1,128]{1,0:T(1,128)S(1)} %get-tuple-element.38.refs_1_, f32[2,512]{1,0:T(2,128)S(1)} %copy-done.8, bf16[3,1536,512]{2,1,0:T(8,128)(2,1)S(1)} %bitcast.29), custom_call_target="tpu_custom_call" | custom-call | flops 1207959552 | bytes 524288 | tf_op jit(solution)/shard_map/conv_w8_512_512/pallas_call | solution.py:557
  54.6 0.0 slice-start.5
  54.7 2.2 %conv_w8_512_512e.1.x_ref = bf16[272,512]{1,0:T(8,128)(2,1)S(1)} custom-call(bf16[288,512]{1,0:T(8,128)(2,1)S(1)} %get-tuple-element.39.refs_0_, f32[1,128]{1,0:T(1,128)S(1)} %get-tuple-element.40.refs_1_, f32[2,512]{1,0:T(2,128)S(1)} %copy-done.7, bf16[3,1536,512]{2,1,0:T(8,128)(2,1)S(1)} %bitcast.32, bf16[272,512]{1,0:T(8,128)(2,1)S(1)} %bitcast.35), custom_call_target="tpu_custom_call" | custom-call | flops 1283457024 | bytes 557056 | tf_op jit(solution)/shard_map/conv_w8_512_512e/pallas_call | solution.py:557
  56.8 0.0 copy-start.17
  56.9 0.0 slice-start.6
  56.9 8.4 %upconv_w16.1 = (bf16[40,2,16,512]{3,2,1,0:T(8,128)(2,1)S(1)}, f32[1,128]{1,0:T(1,128)S(1)}) custom-call(bf16[272,512]{1,0:T(8,128)(2,1)S(1)} %conv_w8_512_512e.1.x_ref, bf16[9,512,512]{2,1,0:T(8,128)(2,1)S(1)} %bitcast.41), custom_call_target="tpu_custom_call" | custom-call | flops 1677721600 | bytes 2621440 | tf_op jit(solution)/shard_map/upconv_w16/pallas_call | solution.py:618
  65.3 0.0 slice-start.7
  65.3 0.0 copy-start.18
  65.3 0.0 slice-start.8
  65.3 12.3 %conv_w16_512_512.1 = (bf16[1088,512]{1,0:T(8,128)(2,1)S(1)}, f32[1,128]{1,0:T(1,128)S(1)}) custom-call(bf16[1280,512]{1,0:T(8,128)(2,1)S(1)} %bitcast.60, f32[1,128]{1,0:T(1,128)S(1)} %get-tuple-element.42.refs_1_, f32[2,512]{1,0:T(2,128)S(1)} %copy-done.17, bf16[3,1536,512]{2,1,0:T(8,128)(2,1)S(1)} %bitcast.44), custom_call_target="tpu_custom_call" | custom-call | flops 4831838208 | bytes 2097152 | tf_op jit(solution)/shard_map/conv_w16_512_512/pallas_call | solution.py:557
  77.7 0.0 slice-start.9
  77.7 6.7 %conv_w16_512_512e.1.x_ref = bf16[1056,512]{1,0:T(8,128)(2,1)S(1)} custom-call(bf16[1088,512]{1,0:T(8,128)(2,1)S(1)} %get-tuple-element.43.refs_0_, f32[1,128]{1,0:T(1,128)S(1)} %get-tuple-element.44.refs_1_, f32[2,512]{1,0:T(2,128)S(1)} %copy-done.18, bf16[3,1536,512]{2,1,0:T(8,128)(2,1)S(1)} %bitcast.47, bf16[1280,512]{1,0:T(8,128)(2,1)S(1)} %bitcast.61), custom_call_target="tpu_custom_call" | custom-call | flops 4982833152 | bytes 2162688 | tf_op jit(solution)/shard_map/conv_w16_512_512e/pallas_call | solution.py:557
  84.5 0.0 copy-start.10
  84.5 0.0 copy-start.15
  84.5 0.0 copy-start.19
  84.5 15.2 %upconv_w32.1 = (bf16[72,2,32,512]{3,2,1,0:T(8,128)(2,1)S(1)}, f32[1,128]{1,0:T(1,128)S(1)}) custom-call(bf16[1056,512]{1,0:T(8,128)(2,1)S(1)} %conv_w16_512_512e.1.x_ref, bf16[9,512,512]{2,1,0:T(8,128)(2,1)S(1)} %bitcast.50), custom_call_target="tpu_custom_call" | custom-call | flops 6039797760 | bytes 9437184 | tf_op jit(solution)/shard_map/upconv_w32/pallas_call | solution.py:618
  99.8 0.0 copy-start.11
  99.8 0.0 copy-start.20
  99.8 17.7 %conv_w32_512_256.1 = (bf16[4224,256]{1,0:T(8,128)(2,1)S(1)}, f32[1,128]{1,0:T(1,128)S(1)}, f32[4160,256]{1,0:T(8,128)S(1)}) custom-call(bf16[4608,512]{1,0:T(8,128)(2,1)S(1)} %bitcast.58, f32[1,128]{1,0:T(1,128)S(1)} %get-tuple-element.46.refs_1_, f32[2,512]{1,0:T(2,128)S(1)} %copy-done.19, bf16[3,1536,256]{2,1,0:T(8,128)(2,1)S(1)} %bitcast.51, ...), custom_call_target="tpu_custom_call" | custom-call | flops 9663676416 | bytes 6291456 | tf_op jit(solution)/shard_map/conv_w32_512_256/pallas_call | solution.py:557
  117.5 0.0 copy-start.12
  117.6 7.1 %conv_w32_256_256e.1.x_ref = bf16[4160,256]{1,0:T(8,128)(2,1)S(1)} custom-call(bf16[4224,256]{1,0:T(8,128)(2,1)S(1)} %get-tuple-element.47.refs_0_, f32[1,128]{1,0:T(1,128)S(1)} %get-tuple-element.48.refs_1_, f32[2,256]{1,0:T(2,128)S(1)} %copy-done.20, bf16[3,768,256]{2,1,0:T(8,128)(2,1)S(1)} %bitcast.52, f32[4160,256]{1,0:T(8,128)S(1)} %get-tuple-element.49.refs_4_), custom_call_target="tpu_custom_call" | custom-call | flops 4907335680 | bytes 4259840 | tf_op jit(solution)/shard_map/conv_w32_256_256e/pallas_call | solution.py:557
  124.6 0.0 copy-start.13
  124.6 0.0 copy-start.16
  124.7 0.0 copy-start.21
  124.7 17.2 %upconv_w64.1 = (bf16[136,2,64,256]{3,2,1,0:T(8,128)(2,1)S(1)}, f32[1,128]{1,0:T(1,128)S(1)}) custom-call(bf16[4160,256]{1,0:T(8,128)(2,1)S(1)} %conv_w32_256_256e.1.x_ref, bf16[9,256,256]{2,1,0:T(8,128)(2,1)S(1)} %bitcast.53), custom_call_target="tpu_custom_call" | custom-call | flops 5704253440 | bytes 17825792 | tf_op jit(solution)/shard_map/upconv_w64/pallas_call | solution.py:618
  141.9 0.0 copy-start.14
  141.9 0.0 copy-start.22
  141.9 23.6 %conv_w64_256_128.1 = (bf16[130,2,64,128]{3,2,1,0:T(8,128)(2,1)S(1)}, f32[1,128]{1,0:T(1,128)S(1)}, f32[17408,128]{1,0:T(8,128)S(1)}) custom-call(bf16[17408,256]{1,0:T(8,128)(2,1)S(1)} %bitcast.57, f32[1,128]{1,0:T(1,128)S(1)} %get-tuple-element.51.refs_1_, f32[2,256]{1,0:T(2,128)S(1)} %copy-done.21, bf16[3,768,128]{2,1,0:T(8,128)(2,1)S(1)} %bitcast.54, ...), custom_call_target="tpu_custom_call" | custom-call | flops 9663676416 | bytes 12582912 | tf_op jit(solution)/shard_map/conv_w64_256_128/pallas_call | solution.py:557
  165.6 0.0 copy-start.23
  165.6 0.0 copy-start.9
  165.6 16.2 %conv_w64_128_128e.1 = (bf16[136,2,64,128]{3,2,1,0:T(8,128)(2,1)S(1)}, f32[1,128]{1,0:T(1,128)S(1)}) custom-call(bf16[16640,128]{1,0:T(8,128)(2,1)S(1)} %bitcast.59, f32[1,128]{1,0:T(1,128)S(1)} %get-tuple-element.53.refs_1_, f32[2,128]{1,0:T(2,128)S(1)} %copy-done.22, bf16[3,384,128]{2,1,0:T(8,128)(2,1)S(1)} %bitcast.55, f32[136,2,64,128]{3,2,1,0:T(8,128)S(1)} %bitcast.56), custom_call_target="tpu_custom_call" | custom-call | flops 4869586944 | bytes 8454144 | tf_op jit(solution)/shard_map/conv_w64_128_128e/pallas_call | solution.py:557
  181.8 12.5 %last_conv.1 = f32[4,96,128]{2,1,0:T(8,128)S(1)} custom-call(bf16[17408,128]{1,0:T(8,128)(2,1)S(1)} %bitcast.33, f32[1,128]{1,0:T(1,128)S(1)} %get-tuple-element.56.tot_ref, f32[2,128]{1,0:T(2,128)S(1)} %copy-done.9, bf16[24,384]{1,0:T(8,128)(2,1)S(1)} %pad_bitcast_fusion.w_ref), custom_call_target="tpu_custom_call" | custom-call | tf_op jit(solution)/shard_map/last_conv/pallas_call | solution.py:690
  194.3 0.4 reshape.130
  194.8 0.4 copy.34
  195.2 0.8 reshape.131
  (44 shorter events, 0.1 us)
Async XLA Ops:
  1.0 53.6 %slice-start = ((s8[4718592]{0:T(1024)(128)(4,1)}), s8[4194304]{0:T(1024)(128)(4,1)S(1)}, s32[]{:S(2)}) async-start(s8[4718592]{0:T(1024)(128)(4,1)} %bitcast.30), calls=%async_computation | async-start | bytes 8388608
  1.0 1.1 copy-start.3
  2.1 1.1 copy-start.5
  3.1 22.3 %copy-start.1 = (bf16[512,1536]{1,0:T(8,128)(2,1)S(1)}, bf16[512,1536]{1,0:T(8,128)(2,1)}, u32[]{:S(2)}) copy-start(bf16[512,1536]{1,0:T(8,128)(2,1)} %wqkv_ref.1) | copy-start | bytes 4718596
  3.1 22.3 %copy-start.2 = (bf16[512,512]{1,0:T(8,128)(2,1)S(1)}, bf16[512,512]{1,0:T(8,128)(2,1)}, u32[]{:S(2)}) copy-start(bf16[512,512]{1,0:T(8,128)(2,1)} %wproj_ref.1) | copy-start | bytes 1572868
  3.1 22.3 %copy-start.4 = (bf16[3,3,16,512]{3,2,1,0:T(8,128)(2,1)S(1)}, bf16[3,3,16,512]{3,2,1,0:T(8,128)(2,1)}, u32[]{:S(2)}) copy-start(bf16[3,3,16,512]{3,2,1,0:T(8,128)(2,1)} %param.39) | copy-start | bytes 442372
  3.1 22.4 %copy-start.6 = (f32[2,512]{1,0:T(2,128)S(1)}, f32[2,512]{1,0:T(2,128)}, u32[]{:S(2)}) copy-start(f32[2,512]{1,0:T(2,128)} %norm_ref.2) | copy-start | bytes 12292
  3.1 43.7 %copy-start = (bf16[3,3,512,512]{3,2,1,0:T(8,128)(2,1)S(1)}, bf16[3,3,512,512]{3,2,1,0:T(8,128)(2,1)}, u32[]{:S(2)}) copy-start(bf16[3,3,512,512]{3,2,1,0:T(8,128)(2,1)} %param.44) | copy-start | bytes 14155780
  3.2 43.7 %copy-start.8 = (f32[2,512]{1,0:T(2,128)S(1)}, f32[2,512]{1,0:T(2,128)}, u32[]{:S(2)}) copy-start(f32[2,512]{1,0:T(2,128)} %refs_2_.8) | copy-start | bytes 12292
  3.2 51.4 %slice-start.1 = ((s8[4718592]{0:T(1024)(128)(4,1)}), s8[524288]{0:T(1024)(128)(4,1)S(1)}, s32[]{:S(2)}) async-start(s8[4718592]{0:T(1024)(128)(4,1)} %bitcast.30), calls=%async_computation.1 | async-start | bytes 1048576
  25.5 29.2 %copy-start.7 = (f32[2,512]{1,0:T(2,128)S(1)}, f32[2,512]{1,0:T(2,128)}, u32[]{:S(2)}) copy-start(f32[2,512]{1,0:T(2,128)} %refs_2_.9) | copy-start | bytes 12292
  25.5 31.3 %slice-start.2 = ((s8[4718592]{0:T(1024)(128)(4,1)}), s8[4194304]{0:T(1024)(128)(4,1)S(1)}, s32[]{:S(2)}) async-start(s8[4718592]{0:T(1024)(128)(4,1)} %bitcast.39), calls=%async_computation.2 | async-start | bytes 8388608
  46.9 10.0 %slice-start.3 = ((s8[4718592]{0:T(1024)(128)(4,1)}), s8[524288]{0:T(1024)(128)(4,1)S(1)}, s32[]{:S(2)}) async-start(s8[4718592]{0:T(1024)(128)(4,1)} %bitcast.39), calls=%async_computation.3 | async-start | bytes 1048576
  46.9 18.4 %slice-start.4 = ((s8[4718592]{0:T(1024)(128)(4,1)}), s8[4194304]{0:T(1024)(128)(4,1)S(1)}, s32[]{:S(2)}) async-start(s8[4718592]{0:T(1024)(128)(4,1)} %bitcast.42), calls=%async_computation.4 | async-start | bytes 8388608
  54.6 10.6 %slice-start.5 = ((s8[4718592]{0:T(1024)(128)(4,1)}), s8[524288]{0:T(1024)(128)(4,1)S(1)}, s32[]{:S(2)}) async-start(s8[4718592]{0:T(1024)(128)(4,1)} %bitcast.42), calls=%async_computation.5 | async-start | bytes 1048576
  56.8 8.5 %copy-start.17 = (f32[2,512]{1,0:T(2,128)S(1)}, f32[2,512]{1,0:T(2,128)}, u32[]{:S(2)}) copy-start(f32[2,512]{1,0:T(2,128)} %refs_2_.10) | copy-start | bytes 12292
  56.9 20.8 %slice-start.6 = ((s8[4718592]{0:T(1024)(128)(4,1)}), s8[4194304]{0:T(1024)(128)(4,1)S(1)}, s32[]{:S(2)}) async-start(s8[4718592]{0:T(1024)(128)(4,1)} %bitcast.45), calls=%async_computation.6 | async-start | bytes 8388608
  65.3 12.4 %slice-start.7 = ((s8[4718592]{0:T(1024)(128)(4,1)}), s8[524288]{0:T(1024)(128)(4,1)S(1)}, s32[]{:S(2)}) async-start(s8[4718592]{0:T(1024)(128)(4,1)} %bitcast.45), calls=%async_computation.7 | async-start | bytes 1048576
  65.3 12.4 %copy-start.18 = (f32[2,512]{1,0:T(2,128)S(1)}, f32[2,512]{1,0:T(2,128)}, u32[]{:S(2)}) copy-start(f32[2,512]{1,0:T(2,128)} %refs_2_.11) | copy-start | bytes 12292
  65.3 19.1 %slice-start.8 = ((s8[4718592]{0:T(1024)(128)(4,1)}), s8[4194304]{0:T(1024)(128)(4,1)S(1)}, s32[]{:S(2)}) async-start(s8[4718592]{0:T(1024)(128)(4,1)} %bitcast.48), calls=%async_computation.8 | async-start | bytes 8388608
  77.7 6.8 %slice-start.9 = ((s8[4718592]{0:T(1024)(128)(4,1)}), s8[524288]{0:T(1024)(128)(4,1)S(1)}, s32[]{:S(2)}) async-start(s8[4718592]{0:T(1024)(128)(4,1)} %bitcast.48), calls=%async_computation.9 | async-start | bytes 1048576
  84.5 15.3 %copy-start.10 = (bf16[3,3,512,256]{3,2,1,0:T(8,128)(2,1)S(1)}, bf16[3,3,512,256]{3,2,1,0:T(8,128)(2,1)}, u32[]{:S(2)}) copy-start(bf16[3,3,512,256]{3,2,1,0:T(8,128)(2,1)} %param.54) | copy-start | bytes 7077892
  84.5 15.3 %copy-start.15 = (bf16[512,256]{1,0:T(8,128)(2,1)S(1)}, bf16[512,256]{1,0:T(8,128)(2,1)}, u32[]{:S(2)}) copy-start(bf16[512,256]{1,0:T(8,128)(2,1)} %refs_4_.2) | copy-start | bytes 786436
  84.5 15.3 %copy-start.19 = (f32[2,512]{1,0:T(2,128)S(1)}, f32[2,512]{1,0:T(2,128)}, u32[]{:S(2)}) copy-start(f32[2,512]{1,0:T(2,128)} %refs_2_.12) | copy-start | bytes 12292
  99.8 17.7 %copy-start.11 = (bf16[3,3,256,256]{3,2,1,0:T(8,128)(2,1)S(1)}, bf16[3,3,256,256]{3,2,1,0:T(8,128)(2,1)}, u32[]{:S(2)}) copy-start(bf16[3,3,256,256]{3,2,1,0:T(8,128)(2,1)} %param.56) | copy-start | bytes 3538948
  99.8 17.7 %copy-start.20 = (f32[2,256]{1,0:T(2,128)S(1)}, f32[2,256]{1,0:T(2,128)}, u32[]{:S(2)}) copy-start(f32[2,256]{1,0:T(2,128)} %refs_2_.13) | copy-start | bytes 6148
  117.5 7.1 %copy-start.12 = (bf16[3,3,256,256]{3,2,1,0:T(8,128)(2,1)S(1)}, bf16[3,3,256,256]{3,2,1,0:T(8,128)(2,1)}, u32[]{:S(2)}) copy-start(bf16[3,3,256,256]{3,2,1,0:T(8,128)(2,1)} %param.58) | copy-start | bytes 3538948
  124.6 17.3 %copy-start.13 = (bf16[3,3,256,128]{3,2,1,0:T(8,128)(2,1)S(1)}, bf16[3,3,256,128]{3,2,1,0:T(8,128)(2,1)}, u32[]{:S(2)}) copy-start(bf16[3,3,256,128]{3,2,1,0:T(8,128)(2,1)} %param.60) | copy-start | bytes 1769476
  124.6 17.3 %copy-start.16 = (bf16[256,128]{1,0:T(8,128)(2,1)S(1)}, bf16[256,128]{1,0:T(8,128)(2,1)}, u32[]{:S(2)}) copy-start(bf16[256,128]{1,0:T(8,128)(2,1)} %refs_4_.3) | copy-start | bytes 196612
  124.7 17.3 %copy-start.21 = (f32[2,256]{1,0:T(2,128)S(1)}, f32[2,256]{1,0:T(2,128)}, u32[]{:S(2)}) copy-start(f32[2,256]{1,0:T(2,128)} %refs_2_.14) | copy-start | bytes 6148
  141.9 23.7 %copy-start.14 = (bf16[3,3,128,128]{3,2,1,0:T(8,128)(2,1)S(1)}, bf16[3,3,128,128]{3,2,1,0:T(8,128)(2,1)}, u32[]{:S(2)}) copy-start(bf16[3,3,128,128]{3,2,1,0:T(8,128)(2,1)} %param.62) | copy-start | bytes 884740
  141.9 23.7 %copy-start.22 = (f32[2,128]{1,0:T(2,128)S(1)}, f32[2,128]{1,0:T(2,128)}, u32[]{:S(2)}) copy-start(f32[2,128]{1,0:T(2,128)} %refs_2_.15) | copy-start | bytes 3076
  165.6 16.2 %copy-start.23 = (bf16[3,3,128,3]{2,3,1,0:T(4,128)(2,1)S(1)}, bf16[3,3,128,3]{2,3,1,0:T(4,128)(2,1)}, u32[]{:S(2)}) copy-start(bf16[3,3,128,3]{2,3,1,0:T(4,128)(2,1)} %param.65) | copy-start | bytes 20740
  165.6 16.2 %copy-start.9 = (f32[2,128]{1,0:T(2,128)S(1)}, f32[2,128]{1,0:T(2,128)}, u32[]{:S(2)}) copy-start(f32[2,128]{1,0:T(2,128)} %norm_ref.3) | copy-start | bytes 3076

commit v2 on v1

--- a/solution.py
+++ b/solution.py
@@ -63,6 +63,7 @@
         self.n = n_row * n_col
         self.row, self.col = lax.axis_index('row'), lax.axis_index('col')
         self.strip = self.row * n_col + self.col
+        self.met = False
 
     def for_others(self, act, row_step=1):
         cols = [lax.rem(self.col + k, self.n_col) for k in range(self.n_col)]
@@ -87,7 +88,9 @@
         self.for_others(lambda device: pl.semaphore_signal(barrier, inc=1, device_id=device, device_id_type=MESH))
 
     def all_here(self):
-        pl.semaphore_wait(pltpu.get_barrier_semaphore(), self.n - 1)
+        if not self.met:
+            pl.semaphore_wait(pltpu.get_barrier_semaphore(), self.n - 1)
+        self.met = True
 
     def to_others(self, src, recv, sems, row_step=1):
         count = self.for_others(lambda device: send(src, recv.at[self.strip], sems, device).start(), row_step)
@@ -221,7 +224,7 @@
                         pltpu.VMEM((2,) + x.shape, BF16), pltpu.VMEM((2,) + x.shape, F32), pltpu.VMEM(x.shape, F32),
                         pltpu.VMEM((n_tok, patch), F32), pltpu.VMEM(lat, F32), pltpu.VMEM((n,) + lat, BF16),
                         pltpu.SemaphoreType.DMA((2, n_buf)), PAIR_SEM, pltpu.SemaphoreType.DMA((2, 2)), pltpu.SemaphoreType.DMA((net_shape[0] // 2, 2))],
-        compiler_params=comm_params(cid, 48),
+        compiler_params=comm_params(cid, 46),
         name='mlp',
     )(x, mod_vec, w_fc1, w_fc2, w_final.T)
 
@@ -451,8 +454,8 @@
         wp_ref[(t + 1) * k:(t + 2) * k, oc:] = w_ref[t]
 
 
-def conv_kernel(cfg, *refs):
-    net_shape, wid, h, blk, out_ext, pair, shortcut, stats, edge, skip_blk = cfg
+def conv_kernel(cfg, net, *refs):
+    wid, h, blk, out_ext, pair, shortcut, stats, edge, skip_blk = cfg
     refs = iter(refs)
     x_ref, norm_tot_ref, norm_ref, w_ref = [next(refs) for _ in 'abcd']
     short_ref = next(refs) if shortcut else None
@@ -463,9 +466,6 @@
     buf0, buf1, s1_ref, s2_ref = [next(refs) for _ in 'abcd']
     wp_ref = next(refs) if pair else w_ref
     net_refs = list(refs)
-    net = Net(*net_shape)
-    if stats:
-        net.greet()
     ch, oc = x_ref.shape[-1], w_ref.shape[2]
     n_out = h + 2 * out_ext
     coefs = norm_coefs(norm_tot_ref[...], norm_ref, ch, float(net.n * h * wid * (ch // GROUPS)))
@@ -532,8 +532,7 @@
         exchange(net, group_sums(s1_ref[...], s2_ref[...]), *net_refs[:3], tot_ref, sides, skip_all if skip_blk else None)
 
 
-def conv(x, tot, norm, w, h, wid, net_shape, blk, out_ext, stats, edge, pair, cid, short, skip):
-    n = net_shape[0] * net_shape[1]
+def conv(x, tot, norm, w, h, wid, n, blk, out_ext, stats, edge, pair, short, skip):
     ch, oc = w.shape[2:]
     args = [x, tot, norm, w.reshape(3, 3 * ch, oc)]
     for src in short:
@@ -544,7 +543,7 @@
     outs = [jax.ShapeDtypeStruct((rows // 2, 2, wid, oc) if pair else (rows * wid, oc), BF16)]
     if stats:
         outs.append(TOTALS)
-    cfg = (net_shape, wid, h, blk, out_ext, pair, bool(short), stats, edge, skip[1] if skip else 0)
+    cfg = (wid, h, blk, out_ext, pair, bool(short), stats, edge, skip[1] if skip else 0)
     if skip:
         outs.append(jax.ShapeDtypeStruct((skip[2] * wid, skip[0].shape[1]), F32))
     layout = Rows(None, x, None, wid, h, None, n_out, blk, pair)
@@ -553,22 +552,11 @@
         scratch.append(pltpu.VMEM((12 * ch, 2 * oc), BF16))
     if stats:
         scratch += net_scratch(n, ((2, wid, oc) if pair else (edge * wid, oc)) if edge else None)
-    px = n_out * wid
-    res = pl.pallas_call(
-        functools.partial(conv_kernel, cfg),
-        out_shape=outs, in_specs=[VMEM_SPEC] * len(args), out_specs=[VMEM_SPEC] * len(outs),
-        scratch_shapes=scratch,
-        compiler_params=comm_params(cid, 28) if stats else pltpu.CompilerParams(vmem_limit_bytes=28 * MIB),
-        cost_estimate=pl.CostEstimate(flops=18 * ch * oc * px, bytes_accessed=2 * px * (ch + oc), transcendentals=px * ch),
-        name='conv_w%d_%d_%d' % (wid, ch, oc) + ('e' if out_ext else ''),
-    )(*args)
-    return [res[0].reshape(rows * wid, oc)] + list(res[1:])
-
-
-def upconv_kernel(cfg, x_ref, w_ref, out_ref, tot_ref, s1_ref, s2_ref, mix_ref, stat_ref, recv, sems):
-    net_shape, half, hs, blk = cfg
-    net = Net(*net_shape)
-    net.greet()
+    return functools.partial(conv_kernel, cfg), args, outs, scratch
+
+
+def upconv_kernel(cfg, net, x_ref, w_ref, out_ref, tot_ref, s1_ref, s2_ref, mix_ref, stat_ref, recv, sems):
+    half, hs, blk = cfg
     oc = w_ref.shape[2]
     n_k = hs + 1
     mixed = half < BASE
@@ -610,22 +598,48 @@
     exchange(net, group_sums(s1_ref[...], s2_ref[...]), stat_ref, recv, sems, tot_ref)
 
 
-def upconv(x, w, hs, half, net_shape, blk, cid):
-    n = net_shape[0] * net_shape[1]
+def upconv(x, w, hs, half, n, blk):
     ch, oc = w.shape[2:]
-    n_k = hs + 8
-    px = 4 * n_k * half
-    out, tot = pl.pallas_call(
-        functools.partial(upconv_kernel, (net_shape, half, hs, blk)),
-        out_shape=[jax.ShapeDtypeStruct((n_k, 2, 2 * half, oc), BF16), TOTALS],
-        in_specs=[VMEM_SPEC] * 2, out_specs=[VMEM_SPEC] * 2,
-        scratch_shapes=[*sum_scratch(oc),
-                        pltpu.VMEM((2, oc // LANES, 2 * blk * half if half < BASE else SUB, LANES), F32)] + net_scratch(n),
-        compiler_params=comm_params(cid, 28),
-        cost_estimate=pl.CostEstimate(flops=5 * ch * oc * px, bytes_accessed=2 * px * (ch + oc), transcendentals=0),
-        name='upconv_w%d' % (2 * half),
-    )(x, w.reshape(9, ch, oc))
-    return out.reshape(px, oc), tot
+    n_k = hs + SUB
+    outs = [jax.ShapeDtypeStruct((n_k, 2, 2 * half, oc), BF16), TOTALS]
+    scratch = [*sum_scratch(oc), pltpu.VMEM((2, oc // LANES, 2 * blk * half if half < BASE else SUB, LANES), F32)]
+    return functools.partial(upconv_kernel, (half, hs, blk)), [x, w.reshape(-1, ch, oc)], outs, scratch + net_scratch(n)
+
+
+class Made:
+    def __init__(self, part, index):
+        self.part, self.index = part, index
+        self.shape = part[2][index].shape
+
+
+def launch(parts, net_shape, cid, mib, name):
+    arrays = []
+    for _, args, _, _ in parts:
+        arrays += [a for a in args if not isinstance(a, Made) and not any(a is b for b in arrays)]
+    outs = parts[-1][2]
+    inner = [o for part in parts[:-1] for o in part[2]]
+
+    def kernel(*refs):
+        refs = iter(refs)
+        given = [next(refs) for _ in arrays]
+        last = [next(refs) for _ in outs]
+        made = [[next(refs) for _ in part[2]] for part in parts[:-1]] + [last]
+        net = Net(*net_shape)
+        net.greet()
+
+        def ref_of(arg):
+            if isinstance(arg, Made):
+                return [refs_[arg.index] for part, refs_ in zip(parts, made) if part is arg.part].pop()
+            return [ref for a, ref in zip(arrays, given) if a is arg].pop()
+        for part, own in zip(parts, made):
+            run, args, _, scratch = part
+            run(net, *[ref_of(a) for a in args], *own, *[next(refs) for _ in scratch])
+        net.all_here()
+    return pl.pallas_call(
+        kernel, out_shape=outs, in_specs=[VMEM_SPEC] * len(arrays), out_specs=[VMEM_SPEC] * len(outs),
+        scratch_shapes=[pltpu.VMEM(o.shape, o.dtype) for o in inner] + [x for part in parts for x in part[3]],
+        compiler_params=comm_params(cid, mib), name=name,
+    )(*arrays)
 
 
 class QuarterRows(Rows):
@@ -707,21 +721,32 @@
     h, wid = 2 * trows, 2 * tok_w
     f, tot = attention(full.reshape(-1, full.shape[-1]), conv_in, norm_attn, w_qkv, w_proj, net_shape, 2)
     u = f.reshape(-1, f.shape[-1])
-    blocks = [(norm0_a, conv0_a, norm0_b, conv0_b, (), upconv_0, h, h + 2, h + 1),
-              (norm1_a, conv1_a, norm1_b, conv1_b, (), upconv_1, 16, 11, 13),
-              (norm2_a, conv2_a, norm2_b, conv2_b, (skip_2,), upconv_2, 16, 10, 10),
-              (norm3_a, conv3_a, norm3_b, conv3_b, (skip_3,), None, 16, 16, 0)]
-    cid = 3
-    for norm_a, conv_a, norm_b, conv_b, skip, up, blk_a, blk_b, blk_up in blocks:
+    blocks = [(norm0_a, conv0_a, norm0_b, conv0_b, (), upconv_0, h, h + 2, h + 1, 15),
+              (norm1_a, conv1_a, norm1_b, conv1_b, (), upconv_1, 16, 11, 13, 13),
+              (norm2_a, conv2_a, norm2_b, conv2_b, (skip_2,), upconv_2, 16, 10, 10, 20),
+              (norm3_a, conv3_a, norm3_b, conv3_b, (skip_3,), None, 16, 16, 0, 24)]
+    cid, n = 3, net_shape[0] * n_col
+    for norm_a, conv_a, norm_b, conv_b, skip, up, blk_a, blk_b, blk_up, mib in blocks:
         last = up is None
-        skip = [(m, blk_b, -(-(h + 2) // blk_b) * blk_b) for m in skip]
-        g, tot, *short = conv(u, tot, norm_a, conv_a, h, wid, net_shape, blk_a, 0, True, 2, last, cid, (), *skip or [()])
-        f, *tot = conv(g, tot, norm_b, conv_b, h, wid, net_shape, blk_b, 1, last, 0, last, cid + 1, short or (u,), ())
-        if not last:
-            u, tot = upconv(f, up, h, wid, net_shape, blk_up, cid + 2)
+        rows = -(-(h + 2) // blk_b) * blk_b
+        skip = [(m, rows // (SUB if rows % SUB == 0 else 5), rows) for m in skip]
+        first = conv(u, tot, norm_a, conv_a, h, wid, n, blk_a, 0, True, 2, last, (), *skip or [()])
+        name = 'level_w%d' % wid
+        if last:
+            g, tot, *short = launch([first], net_shape, cid, mib, name + 'a')
+            g, short = g.reshape(-1, g.shape[-1]), short
+        else:
+            g, tot, *short = [Made(first, i) for i, _ in enumerate(first[2])]
+        second = conv(g, tot, norm_b, conv_b, h, wid, n, blk_b, 1, last, 0, last, short or (u,), ())
+        if last:
+            f, tot = launch([second], net_shape, cid + 1, mib, name + 'b')
+        else:
+            third = upconv(Made(second, 0), up, h, wid, n, blk_up)
+            u, tot = launch([first, second, third], net_shape, cid, mib, name)
+            u = u.reshape(-1, u.shape[-1])
             h, wid = 2 * h, 2 * wid
-        cid += 3
-    tile = last_conv(f, tot[0], norm_out, conv_out, h, wid, net_shape, 16, cid)
+        cid += 2
+    tile = last_conv(f.reshape(-1, f.shape[-1]), tot, norm_out, conv_out, h, wid, net_shape, 16, cid)
     tile = tile.reshape(n_col, -1, h, wid // n_col).transpose(0, 2, 3, 1)
     return tile.reshape(n_col * h, wid // n_col, -1)
 

time: 196 us -> 193 us (0.985)
  Pallas kernels: 190 us -> 187 us
    pallas_call x11 -> x5, Pallas kernels: 134 us -> 130 us  [launch(): pl.pallas_call(kernel, out_shape=outs, in_specs=[VMEM_SPEC] * len(arrays)...]
where the time goes in v2:
time: 193 us
  Pallas kernels  187 us (97%)
  local copies, waits for them, and re-layouts  5.28 us (3%)
    pallas_call x5, Pallas kernels, launch(): pl.pallas_call(kernel, out_shape=outs, in_specs=[VMEM_SPEC] * len(arrays)...  130 us
    pallas_call x1, Pallas kernels, mlp(): pl.pallas_call(functools.partial(mlp_kernel, net_shape), out_shape=jax.Sh...  22.3 us
    pallas_call x1, Pallas kernels, attention(): pl.pallas_call(functools.partial(attention_kernel, net_shape), out_shape=...  21.3 us
    pallas_call x1, Pallas kernels, last_conv(): pl.pallas_call(functools.partial(last_kernel, (net_shape, wid, h, blk, oc...  12.8 us

profile of v2, /device:TPU:97, one launch (start us, length us, event | category | flops | bytes accessed | tf_op | source)
XLA Modules:
  0.0 192.7 jit_solution(2615590807005533446)
XLA Ops:
  0.0 1.0 reshape.107.x_ref
  1.0 0.0 slice-start
  1.0 0.0 slice-start.2
  1.0 0.0 slice-start.4
  1.0 0.0 copy-start.9
  1.0 1.1 copy-done.9
  2.1 1.4 copy-done.12
  3.5 0.0 slice-start.1
  3.5 0.0 slice-start.3
  3.5 0.0 slice-start.5
  3.5 0.0 copy-start.15
  3.5 0.0 copy-start.16
  3.5 22.3 %mlp.1 = bf16[32,32,128]{2,1,0:T(8,128)(2,1)S(1)} custom-call(bf16[64,1536]{1,0:T(8,128)(2,1)S(1)} %reshape.107.x_ref, f32[5,1536]{1,0:T(8,128)S(1)} %copy-done.12, bf16[1536,6144]{1,0:T(8,128)(2,1)} %w1_ref.1, bf16[6144,1536]{1,0:T(8,128)(2,1)} %w2_ref.1, bf16[64,1536]{1,0:T(8,128)(2,1)S(1)} %bitcast.58), custom_call_target="tpu_custom_call" | custom-call | tf_op jit(solution)/shard_map/mlp/pallas_call | solution.py:218
  25.8 0.0 copy-done.2
  25.8 0.0 copy-done.6
  25.8 0.0 copy-done.10
  25.8 0.0 copy-done.14
  25.8 0.0 slice-start.6
  25.8 0.0 slice-start.8
  25.9 21.3 %attention.1 = (bf16[34,8,512]{2,1,0:T(8,128)(2,1)S(1)}, f32[1,128]{1,0:T(1,128)S(1)}) custom-call(bf16[1024,128]{1,0:T(8,128)(2,1)S(1)} %bitcast.54, bf16[9,16,512]{2,1,0:T(8,128)(2,1)S(1)} %bitcast.59, f32[2,512]{1,0:T(2,128)S(1)} %copy-done.14, bf16[512,1536]{1,0:T(8,128)(2,1)S(1)} %copy-done.2, bf16[512,512]{1,0:T(8,128)(2,1)S(1)} %copy-done.6), custom_call_target="tpu_custom_call" | custom-call | tf_op jit(solution)/shard_map/attention/pallas_call | solution.py:341
  47.2 0.0 slice-done
  47.3 0.0 slice-start.7
  47.3 0.0 slice-start.9
  47.3 0.0 copy-start
  47.3 0.0 copy-start.17
  47.4 0.0 copy-start.18
  47.4 17.3 %level_w8.1 = (bf16[40,2,16,512]{3,2,1,0:T(8,128)(2,1)S(1)}, f32[1,128]{1,0:T(1,128)S(1)}) custom-call(bf16[272,512]{1,0:T(8,128)(2,1)S(1)} %bitcast.57, f32[1,128]{1,0:T(1,128)S(1)} %get-tuple-element.31.refs_1_, f32[2,512]{1,0:T(2,128)S(1)} %copy-done.15, bf16[3,1536,512]{2,1,0:T(8,128)(2,1)S(1)} %bitcast.33, f32[2,512]{1,0:T(2,128)S(1)} %copy-done.16, ...), custom_call_target="tpu_custom_call" | custom-call | tf_op jit(solution)/shard_map/level_w8/pallas_call | solution.py:638
  64.7 0.0 copy-start.1
  64.7 0.0 copy-start.3
  64.7 0.0 copy-start.4
  64.7 0.0 copy-start.8
  64.8 0.0 copy-start.13
  64.8 0.0 copy-start.19
  64.8 33.1 %level_w16.1 = (bf16[72,2,32,512]{3,2,1,0:T(8,128)(2,1)S(1)}, f32[1,128]{1,0:T(1,128)S(1)}) custom-call(bf16[1280,512]{1,0:T(8,128)(2,1)S(1)} %bitcast.51, f32[1,128]{1,0:T(1,128)S(1)} %get-tuple-element.33.refs_1_, f32[2,512]{1,0:T(2,128)S(1)} %copy-done.17, bf16[3,1536,512]{2,1,0:T(8,128)(2,1)S(1)} %bitcast.43, f32[2,512]{1,0:T(2,128)S(1)} %copy-done.18, ...), custom_call_target="tpu_custom_call" | custom-call | tf_op jit(solution)/shard_map/level_w16/pallas_call | solution.py:638
  97.9 0.0 copy-start.5
  98.0 0.0 copy-start.11
  98.0 0.0 copy-start.20
  98.0 41.5 %level_w32.1 = (bf16[136,2,64,256]{3,2,1,0:T(8,128)(2,1)S(1)}, f32[1,128]{1,0:T(1,128)S(1)}) custom-call(bf16[4608,512]{1,0:T(8,128)(2,1)S(1)} %bitcast.40, f32[1,128]{1,0:T(1,128)S(1)} %get-tuple-element.35.refs_1_, f32[2,512]{1,0:T(2,128)S(1)} %copy-done.13, bf16[3,1536,256]{2,1,0:T(8,128)(2,1)S(1)} %bitcast.50, bf16[512,256]{1,0:T(8,128)(2,1)S(1)} %copy-done.8, ...), custom_call_target="tpu_custom_call" | custom-call | tf_op jit(solution)/shard_map/level_w32/pallas_call | solution.py:638
  139.5 0.0 copy-start.7
  139.5 0.0 copy-start.21
  139.5 22.8 %level_w64a.1 = (bf16[130,2,64,128]{3,2,1,0:T(8,128)(2,1)S(1)}, f32[1,128]{1,0:T(1,128)S(1)}, f32[17408,128]{1,0:T(8,128)S(1)}) custom-call(bf16[17408,256]{1,0:T(8,128)(2,1)S(1)} %bitcast.29, f32[1,128]{1,0:T(1,128)S(1)} %get-tuple-element.37.refs_1_, f32[2,256]{1,0:T(2,128)S(1)} %copy-done.20, bf16[3,768,128]{2,1,0:T(8,128)(2,1)S(1)} %bitcast.55, ...), custom_call_target="tpu_custom_call" | custom-call | tf_op jit(solution)/shard_map/level_w64a/pallas_call | solution.py:638
  162.3 0.0 copy-start.23
  162.3 0.0 copy-start.22
  162.3 15.8 %level_w64b.1 = (bf16[136,2,64,128]{3,2,1,0:T(8,128)(2,1)S(1)}, f32[1,128]{1,0:T(1,128)S(1)}) custom-call(bf16[16640,128]{1,0:T(8,128)(2,1)S(1)} %bitcast.49, f32[1,128]{1,0:T(1,128)S(1)} %get-tuple-element.39.refs_1_, f32[2,128]{1,0:T(2,128)S(1)} %copy-done.21, bf16[3,384,128]{2,1,0:T(8,128)(2,1)S(1)} %bitcast.56, f32[136,2,64,128]{3,2,1,0:T(8,128)S(1)} %bitcast.30), custom_call_target="tpu_custom_call" | custom-call | tf_op jit(solution)/shard_map/level_w64b/pallas_call | solution.py:638
  178.2 12.8 %last_conv.1 = f32[4,96,128]{2,1,0:T(8,128)S(1)} custom-call(bf16[17408,128]{1,0:T(8,128)(2,1)S(1)} %bitcast.48, f32[1,128]{1,0:T(1,128)S(1)} %get-tuple-element.42.tot_ref, f32[2,128]{1,0:T(2,128)S(1)} %copy-done.22, bf16[24,384]{1,0:T(8,128)(2,1)S(1)} %pad_bitcast_fusion.w_ref), custom_call_target="tpu_custom_call" | custom-call | tf_op jit(solution)/shard_map/last_conv/pallas_call | solution.py:704
  191.0 0.4 reshape.130
  191.5 0.4 copy.34
  191.9 0.8 reshape.131
  (38 shorter events, 0.1 us)
Async XLA Ops:
  1.0 46.2 %slice-start = ((s8[4718592]{0:T(1024)(128)(4,1)}), s8[4194304]{0:T(1024)(128)(4,1)S(1)}, s32[]{:S(2)}) async-start(s8[4718592]{0:T(1024)(128)(4,1)} %bitcast.31), calls=%async_computation | async-start | bytes 8388608
  1.0 46.2 %slice-start.2 = ((s8[4718592]{0:T(1024)(128)(4,1)}), s8[4194304]{0:T(1024)(128)(4,1)S(1)}, s32[]{:S(2)}) async-start(s8[4718592]{0:T(1024)(128)(4,1)} %bitcast.34), calls=%async_computation.2 | async-start | bytes 8388608
  1.0 46.2 %slice-start.4 = ((s8[4718592]{0:T(1024)(128)(4,1)}), s8[4194304]{0:T(1024)(128)(4,1)S(1)}, s32[]{:S(2)}) async-start(s8[4718592]{0:T(1024)(128)(4,1)} %bitcast.37), calls=%async_computation.4 | async-start | bytes 8388608
  1.0 1.1 copy-start.9
  2.1 1.4 copy-start.12
  3.5 22.3 %copy-start.2 = (bf16[512,1536]{1,0:T(8,128)(2,1)S(1)}, bf16[512,1536]{1,0:T(8,128)(2,1)}, u32[]{:S(2)}) copy-start(bf16[512,1536]{1,0:T(8,128)(2,1)} %wqkv_ref.1) | copy-start | bytes 4718596
  3.5 22.3 %copy-start.6 = (bf16[512,512]{1,0:T(8,128)(2,1)S(1)}, bf16[512,512]{1,0:T(8,128)(2,1)}, u32[]{:S(2)}) copy-start(bf16[512,512]{1,0:T(8,128)(2,1)} %wproj_ref.1) | copy-start | bytes 1572868
  3.5 22.4 %copy-start.10 = (bf16[3,3,16,512]{3,2,1,0:T(8,128)(2,1)S(1)}, bf16[3,3,16,512]{3,2,1,0:T(8,128)(2,1)}, u32[]{:S(2)}) copy-start(bf16[3,3,16,512]{3,2,1,0:T(8,128)(2,1)} %param.39) | copy-start | bytes 442372
  3.5 22.4 %copy-start.14 = (f32[2,512]{1,0:T(2,128)S(1)}, f32[2,512]{1,0:T(2,128)}, u32[]{:S(2)}) copy-start(f32[2,512]{1,0:T(2,128)} %norm_ref.2) | copy-start | bytes 12292
  3.5 43.8 %slice-start.1 = ((s8[4718592]{0:T(1024)(128)(4,1)}), s8[524288]{0:T(1024)(128)(4,1)S(1)}, s32[]{:S(2)}) async-start(s8[4718592]{0:T(1024)(128)(4,1)} %bitcast.31), calls=%async_computation.1 | async-start | bytes 1048576
  3.5 43.8 %slice-start.3 = ((s8[4718592]{0:T(1024)(128)(4,1)}), s8[524288]{0:T(1024)(128)(4,1)S(1)}, s32[]{:S(2)}) async-start(s8[4718592]{0:T(1024)(128)(4,1)} %bitcast.34), calls=%async_computation.3 | async-start | bytes 1048576
  3.5 43.8 %slice-start.5 = ((s8[4718592]{0:T(1024)(128)(4,1)}), s8[524288]{0:T(1024)(128)(4,1)S(1)}, s32[]{:S(2)}) async-start(s8[4718592]{0:T(1024)(128)(4,1)} %bitcast.37), calls=%async_computation.5 | async-start | bytes 1048576
  3.5 43.8 %copy-start.15 = (f32[2,512]{1,0:T(2,128)S(1)}, f32[2,512]{1,0:T(2,128)}, u32[]{:S(2)}) copy-start(f32[2,512]{1,0:T(2,128)} %refs_2_.5) | copy-start | bytes 12292
  3.5 43.8 %copy-start.16 = (f32[2,512]{1,0:T(2,128)S(1)}, f32[2,512]{1,0:T(2,128)}, u32[]{:S(2)}) copy-start(f32[2,512]{1,0:T(2,128)} %refs_4_.4) | copy-start | bytes 12292
  25.8 38.8 %slice-start.6 = ((s8[4718592]{0:T(1024)(128)(4,1)}), s8[4194304]{0:T(1024)(128)(4,1)S(1)}, s32[]{:S(2)}) async-start(s8[4718592]{0:T(1024)(128)(4,1)} %bitcast.41), calls=%async_computation.6 | async-start | bytes 8388608
  25.8 38.8 %slice-start.8 = ((s8[4718592]{0:T(1024)(128)(4,1)}), s8[4194304]{0:T(1024)(128)(4,1)S(1)}, s32[]{:S(2)}) async-start(s8[4718592]{0:T(1024)(128)(4,1)} %bitcast.44), calls=%async_computation.8 | async-start | bytes 8388608
  47.3 17.3 %slice-start.7 = ((s8[4718592]{0:T(1024)(128)(4,1)}), s8[524288]{0:T(1024)(128)(4,1)S(1)}, s32[]{:S(2)}) async-start(s8[4718592]{0:T(1024)(128)(4,1)} %bitcast.41), calls=%async_computation.7 | async-start | bytes 1048576
  47.3 17.3 %slice-start.9 = ((s8[4718592]{0:T(1024)(128)(4,1)}), s8[524288]{0:T(1024)(128)(4,1)S(1)}, s32[]{:S(2)}) async-start(s8[4718592]{0:T(1024)(128)(4,1)} %bitcast.44), calls=%async_computation.9 | async-start | bytes 1048576
  47.3 17.3 %copy-start = (bf16[3,3,512,512]{3,2,1,0:T(8,128)(2,1)S(1)}, bf16[3,3,512,512]{3,2,1,0:T(8,128)(2,1)}, u32[]{:S(2)}) copy-start(bf16[3,3,512,512]{3,2,1,0:T(8,128)(2,1)} %param.52) | copy-start | bytes 14155780
  47.3 17.3 %copy-start.17 = (f32[2,512]{1,0:T(2,128)S(1)}, f32[2,512]{1,0:T(2,128)}, u32[]{:S(2)}) copy-start(f32[2,512]{1,0:T(2,128)} %refs_2_.6) | copy-start | bytes 12292
  47.4 17.3 %copy-start.18 = (f32[2,512]{1,0:T(2,128)S(1)}, f32[2,512]{1,0:T(2,128)}, u32[]{:S(2)}) copy-start(f32[2,512]{1,0:T(2,128)} %refs_4_.5) | copy-start | bytes 12292
  64.7 33.2 %copy-start.1 = (bf16[3,3,512,256]{3,2,1,0:T(8,128)(2,1)S(1)}, bf16[3,3,512,256]{3,2,1,0:T(8,128)(2,1)}, u32[]{:S(2)}) copy-start(bf16[3,3,512,256]{3,2,1,0:T(8,128)(2,1)} %param.54) | copy-start | bytes 7077892
  64.7 33.2 %copy-start.3 = (bf16[3,3,256,256]{3,2,1,0:T(8,128)(2,1)S(1)}, bf16[3,3,256,256]{3,2,1,0:T(8,128)(2,1)}, u32[]{:S(2)}) copy-start(bf16[3,3,256,256]{3,2,1,0:T(8,128)(2,1)} %param.56) | copy-start | bytes 3538948
  64.7 33.2 %copy-start.4 = (bf16[3,3,256,256]{3,2,1,0:T(8,128)(2,1)S(1)}, bf16[3,3,256,256]{3,2,1,0:T(8,128)(2,1)}, u32[]{:S(2)}) copy-start(bf16[3,3,256,256]{3,2,1,0:T(8,128)(2,1)} %param.58) | copy-start | bytes 3538948
  64.7 33.2 %copy-start.8 = (bf16[512,256]{1,0:T(8,128)(2,1)S(1)}, bf16[512,256]{1,0:T(8,128)(2,1)}, u32[]{:S(2)}) copy-start(bf16[512,256]{1,0:T(8,128)(2,1)} %refs_4_.6) | copy-start | bytes 786436
  64.8 33.2 %copy-start.13 = (f32[2,512]{1,0:T(2,128)S(1)}, f32[2,512]{1,0:T(2,128)}, u32[]{:S(2)}) copy-start(f32[2,512]{1,0:T(2,128)} %refs_2_.7) | copy-start | bytes 12292
  64.8 33.2 %copy-start.19 = (f32[2,256]{1,0:T(2,128)S(1)}, f32[2,256]{1,0:T(2,128)}, u32[]{:S(2)}) copy-start(f32[2,256]{1,0:T(2,128)} %refs_5_.1) | copy-start | bytes 6148
  97.9 41.5 %copy-start.5 = (bf16[3,3,256,128]{3,2,1,0:T(8,128)(2,1)S(1)}, bf16[3,3,256,128]{3,2,1,0:T(8,128)(2,1)}, u32[]{:S(2)}) copy-start(bf16[3,3,256,128]{3,2,1,0:T(8,128)(2,1)} %param.60) | copy-start | bytes 1769476
  98.0 41.5 %copy-start.11 = (bf16[256,128]{1,0:T(8,128)(2,1)S(1)}, bf16[256,128]{1,0:T(8,128)(2,1)}, u32[]{:S(2)}) copy-start(bf16[256,128]{1,0:T(8,128)(2,1)} %refs_4_.7) | copy-start | bytes 196612
  98.0 41.5 %copy-start.20 = (f32[2,256]{1,0:T(2,128)S(1)}, f32[2,256]{1,0:T(2,128)}, u32[]{:S(2)}) copy-start(f32[2,256]{1,0:T(2,128)} %refs_2_.8) | copy-start | bytes 6148
  139.5 22.8 %copy-start.7 = (bf16[3,3,128,128]{3,2,1,0:T(8,128)(2,1)S(1)}, bf16[3,3,128,128]{3,2,1,0:T(8,128)(2,1)}, u32[]{:S(2)}) copy-start(bf16[3,3,128,128]{3,2,1,0:T(8,128)(2,1)} %param.62) | copy-start | bytes 884740
  139.5 22.8 %copy-start.21 = (f32[2,128]{1,0:T(2,128)S(1)}, f32[2,128]{1,0:T(2,128)}, u32[]{:S(2)}) copy-start(f32[2,128]{1,0:T(2,128)} %refs_2_.9) | copy-start | bytes 3076
  162.3 15.9 %copy-start.23 = (bf16[3,3,128,3]{2,3,1,0:T(4,128)(2,1)S(1)}, bf16[3,3,128,3]{2,3,1,0:T(4,128)(2,1)}, u32[]{:S(2)}) copy-start(bf16[3,3,128,3]{2,3,1,0:T(4,128)(2,1)} %param.65) | copy-start | bytes 20740
  162.3 15.9 %copy-start.22 = (f32[2,128]{1,0:T(2,128)S(1)}, f32[2,128]{1,0:T(2,128)}, u32[]{:S(2)}) copy-start(f32[2,128]{1,0:T(2,128)} %norm_ref.3) | copy-start | bytes 3076

commit v3 on v2

--- a/solution.py
+++ b/solution.py
@@ -722,8 +722,8 @@
     f, tot = attention(full.reshape(-1, full.shape[-1]), conv_in, norm_attn, w_qkv, w_proj, net_shape, 2)
     u = f.reshape(-1, f.shape[-1])
     blocks = [(norm0_a, conv0_a, norm0_b, conv0_b, (), upconv_0, h, h + 2, h + 1, 15),
-              (norm1_a, conv1_a, norm1_b, conv1_b, (), upconv_1, 16, 11, 13, 13),
-              (norm2_a, conv2_a, norm2_b, conv2_b, (skip_2,), upconv_2, 16, 10, 10, 20),
+              (norm1_a, conv1_a, norm1_b, conv1_b, (), upconv_1, 16, 22, 13, 13),
+              (norm2_a, conv2_a, norm2_b, conv2_b, (skip_2,), upconv_2, 16, 13, 10, 20),
               (norm3_a, conv3_a, norm3_b, conv3_b, (skip_3,), None, 16, 16, 0, 24)]
     cid, n = 3, net_shape[0] * n_col
     for norm_a, conv_a, norm_b, conv_b, skip, up, blk_a, blk_b, blk_up, mib in blocks:

time: 193 us -> 192 us (level)
  no operation moved by 1% of the time
where the time goes in v3:
time: 192 us
  Pallas kernels  186 us (97%)
  local copies, waits for them, and re-layouts  5.28 us (3%)
    pallas_call x5, Pallas kernels, launch(): pl.pallas_call(kernel, out_shape=outs, in_specs=[VMEM_SPEC] * len(arrays)...  130 us
    pallas_call x1, Pallas kernels, mlp(): pl.pallas_call(functools.partial(mlp_kernel, net_shape), out_shape=jax.Sh...  22.3 us
    pallas_call x1, Pallas kernels, attention(): pl.pallas_call(functools.partial(attention_kernel, net_shape), out_shape=...  21.3 us
    pallas_call x1, Pallas kernels, last_conv(): pl.pallas_call(functools.partial(last_kernel, (net_shape, wid, h, blk, oc...  12.8 us

profile of v3, /device:TPU:97, one launch (start us, length us, event | category | flops | bytes accessed | tf_op | source)
XLA Modules:
  0.0 191.8 jit_solution(9229377070848157053)
XLA Ops:
  0.0 1.0 reshape.107.x_ref
  1.0 0.0 slice-start
  1.0 0.0 slice-start.2
  1.0 0.0 slice-start.4
  1.0 0.0 copy-start.9
  1.0 1.1 copy-done.9
  2.1 1.4 copy-done.12
  3.5 0.0 slice-start.1
  3.5 0.0 slice-start.3
  3.5 0.0 slice-start.5
  3.5 0.0 copy-start.15
  3.5 0.0 copy-start.16
  3.5 22.3 %mlp.1 = bf16[32,32,128]{2,1,0:T(8,128)(2,1)S(1)} custom-call(bf16[64,1536]{1,0:T(8,128)(2,1)S(1)} %reshape.107.x_ref, f32[5,1536]{1,0:T(8,128)S(1)} %copy-done.12, bf16[1536,6144]{1,0:T(8,128)(2,1)} %w1_ref.1, bf16[6144,1536]{1,0:T(8,128)(2,1)} %w2_ref.1, bf16[64,1536]{1,0:T(8,128)(2,1)S(1)} %bitcast.58), custom_call_target="tpu_custom_call" | custom-call | tf_op jit(solution)/shard_map/mlp/pallas_call | solution.py:218
  25.8 0.0 copy-done.2
  25.8 0.0 copy-done.6
  25.8 0.0 copy-done.10
  25.8 0.0 copy-done.14
  25.8 0.0 slice-start.6
  25.8 0.0 slice-start.8
  25.9 21.3 %attention.1 = (bf16[34,8,512]{2,1,0:T(8,128)(2,1)S(1)}, f32[1,128]{1,0:T(1,128)S(1)}) custom-call(bf16[1024,128]{1,0:T(8,128)(2,1)S(1)} %bitcast.54, bf16[9,16,512]{2,1,0:T(8,128)(2,1)S(1)} %bitcast.59, f32[2,512]{1,0:T(2,128)S(1)} %copy-done.14, bf16[512,1536]{1,0:T(8,128)(2,1)S(1)} %copy-done.2, bf16[512,512]{1,0:T(8,128)(2,1)S(1)} %copy-done.6), custom_call_target="tpu_custom_call" | custom-call | tf_op jit(solution)/shard_map/attention/pallas_call | solution.py:341
  47.2 0.0 slice-done
  47.3 0.0 slice-start.7
  47.3 0.0 slice-start.9
  47.3 0.0 copy-start
  47.3 0.0 copy-start.17
  47.4 0.0 copy-start.18
  47.4 17.3 %level_w8.1 = (bf16[40,2,16,512]{3,2,1,0:T(8,128)(2,1)S(1)}, f32[1,128]{1,0:T(1,128)S(1)}) custom-call(bf16[272,512]{1,0:T(8,128)(2,1)S(1)} %bitcast.57, f32[1,128]{1,0:T(1,128)S(1)} %get-tuple-element.31.refs_1_, f32[2,512]{1,0:T(2,128)S(1)} %copy-done.15, bf16[3,1536,512]{2,1,0:T(8,128)(2,1)S(1)} %bitcast.33, f32[2,512]{1,0:T(2,128)S(1)} %copy-done.16, ...), custom_call_target="tpu_custom_call" | custom-call | tf_op jit(solution)/shard_map/level_w8/pallas_call | solution.py:638
  64.7 0.0 copy-start.1
  64.7 0.0 copy-start.3
  64.7 0.0 copy-start.4
  64.7 0.0 copy-start.8
  64.8 0.0 copy-start.13
  64.8 0.0 copy-start.19
  64.8 32.5 %level_w16.1 = (bf16[72,2,32,512]{3,2,1,0:T(8,128)(2,1)S(1)}, f32[1,128]{1,0:T(1,128)S(1)}) custom-call(bf16[1280,512]{1,0:T(8,128)(2,1)S(1)} %bitcast.51, f32[1,128]{1,0:T(1,128)S(1)} %get-tuple-element.33.refs_1_, f32[2,512]{1,0:T(2,128)S(1)} %copy-done.17, bf16[3,1536,512]{2,1,0:T(8,128)(2,1)S(1)} %bitcast.43, f32[2,512]{1,0:T(2,128)S(1)} %copy-done.18, ...), custom_call_target="tpu_custom_call" | custom-call | tf_op jit(solution)/shard_map/level_w16/pallas_call | solution.py:638
  97.3 0.0 copy-start.5
  97.3 0.0 copy-start.11
  97.3 0.0 copy-start.20
  97.4 41.2 %level_w32.1 = (bf16[136,2,64,256]{3,2,1,0:T(8,128)(2,1)S(1)}, f32[1,128]{1,0:T(1,128)S(1)}) custom-call(bf16[4608,512]{1,0:T(8,128)(2,1)S(1)} %bitcast.40, f32[1,128]{1,0:T(1,128)S(1)} %get-tuple-element.35.refs_1_, f32[2,512]{1,0:T(2,128)S(1)} %copy-done.13, bf16[3,1536,256]{2,1,0:T(8,128)(2,1)S(1)} %bitcast.50, bf16[512,256]{1,0:T(8,128)(2,1)S(1)} %copy-done.8, ...), custom_call_target="tpu_custom_call" | custom-call | tf_op jit(solution)/shard_map/level_w32/pallas_call | solution.py:638
  138.6 0.0 copy-start.7
  138.6 0.0 copy-start.21
  138.6 22.8 %level_w64a.1 = (bf16[130,2,64,128]{3,2,1,0:T(8,128)(2,1)S(1)}, f32[1,128]{1,0:T(1,128)S(1)}, f32[17408,128]{1,0:T(8,128)S(1)}) custom-call(bf16[17408,256]{1,0:T(8,128)(2,1)S(1)} %bitcast.29, f32[1,128]{1,0:T(1,128)S(1)} %get-tuple-element.37.refs_1_, f32[2,256]{1,0:T(2,128)S(1)} %copy-done.20, bf16[3,768,128]{2,1,0:T(8,128)(2,1)S(1)} %bitcast.55, ...), custom_call_target="tpu_custom_call" | custom-call | tf_op jit(solution)/shard_map/level_w64a/pallas_call | solution.py:638
  161.4 0.0 copy-start.23
  161.4 0.0 copy-start.22
  161.4 15.8 %level_w64b.1 = (bf16[136,2,64,128]{3,2,1,0:T(8,128)(2,1)S(1)}, f32[1,128]{1,0:T(1,128)S(1)}) custom-call(bf16[16640,128]{1,0:T(8,128)(2,1)S(1)} %bitcast.49, f32[1,128]{1,0:T(1,128)S(1)} %get-tuple-element.39.refs_1_, f32[2,128]{1,0:T(2,128)S(1)} %copy-done.21, bf16[3,384,128]{2,1,0:T(8,128)(2,1)S(1)} %bitcast.56, f32[136,2,64,128]{3,2,1,0:T(8,128)S(1)} %bitcast.30), custom_call_target="tpu_custom_call" | custom-call | tf_op jit(solution)/shard_map/level_w64b/pallas_call | solution.py:638
  177.3 12.8 %last_conv.1 = f32[4,96,128]{2,1,0:T(8,128)S(1)} custom-call(bf16[17408,128]{1,0:T(8,128)(2,1)S(1)} %bitcast.48, f32[1,128]{1,0:T(1,128)S(1)} %get-tuple-element.42.tot_ref, f32[2,128]{1,0:T(2,128)S(1)} %copy-done.22, bf16[24,384]{1,0:T(8,128)(2,1)S(1)} %pad_bitcast_fusion.w_ref), custom_call_target="tpu_custom_call" | custom-call | tf_op jit(solution)/shard_map/last_conv/pallas_call | solution.py:704
  190.1 0.4 reshape.130
  190.5 0.4 copy.34
  191.0 0.8 reshape.131
  (38 shorter events, 0.1 us)
Async XLA Ops:
  1.0 46.2 %slice-start = ((s8[4718592]{0:T(1024)(128)(4,1)}), s8[4194304]{0:T(1024)(128)(4,1)S(1)}, s32[]{:S(2)}) async-start(s8[4718592]{0:T(1024)(128)(4,1)} %bitcast.31), calls=%async_computation | async-start | bytes 8388608
  1.0 46.2 %slice-start.2 = ((s8[4718592]{0:T(1024)(128)(4,1)}), s8[4194304]{0:T(1024)(128)(4,1)S(1)}, s32[]{:S(2)}) async-start(s8[4718592]{0:T(1024)(128)(4,1)} %bitcast.34), calls=%async_computation.2 | async-start | bytes 8388608
  1.0 46.2 %slice-start.4 = ((s8[4718592]{0:T(1024)(128)(4,1)}), s8[4194304]{0:T(1024)(128)(4,1)S(1)}, s32[]{:S(2)}) async-start(s8[4718592]{0:T(1024)(128)(4,1)} %bitcast.37), calls=%async_computation.4 | async-start | bytes 8388608
  1.0 1.1 copy-start.9
  2.1 1.4 copy-start.12
  3.5 22.3 %copy-start.2 = (bf16[512,1536]{1,0:T(8,128)(2,1)S(1)}, bf16[512,1536]{1,0:T(8,128)(2,1)}, u32[]{:S(2)}) copy-start(bf16[512,1536]{1,0:T(8,128)(2,1)} %wqkv_ref.1) | copy-start | bytes 4718596
  3.5 22.3 %copy-start.6 = (bf16[512,512]{1,0:T(8,128)(2,1)S(1)}, bf16[512,512]{1,0:T(8,128)(2,1)}, u32[]{:S(2)}) copy-start(bf16[512,512]{1,0:T(8,128)(2,1)} %wproj_ref.1) | copy-start | bytes 1572868
  3.5 22.4 %copy-start.10 = (bf16[3,3,16,512]{3,2,1,0:T(8,128)(2,1)S(1)}, bf16[3,3,16,512]{3,2,1,0:T(8,128)(2,1)}, u32[]{:S(2)}) copy-start(bf16[3,3,16,512]{3,2,1,0:T(8,128)(2,1)} %param.39) | copy-start | bytes 442372
  3.5 22.4 %copy-start.14 = (f32[2,512]{1,0:T(2,128)S(1)}, f32[2,512]{1,0:T(2,128)}, u32[]{:S(2)}) copy-start(f32[2,512]{1,0:T(2,128)} %norm_ref.2) | copy-start | bytes 12292
  3.5 43.8 %slice-start.1 = ((s8[4718592]{0:T(1024)(128)(4,1)}), s8[524288]{0:T(1024)(128)(4,1)S(1)}, s32[]{:S(2)}) async-start(s8[4718592]{0:T(1024)(128)(4,1)} %bitcast.31), calls=%async_computation.1 | async-start | bytes 1048576
  3.5 43.8 %slice-start.3 = ((s8[4718592]{0:T(1024)(128)(4,1)}), s8[524288]{0:T(1024)(128)(4,1)S(1)}, s32[]{:S(2)}) async-start(s8[4718592]{0:T(1024)(128)(4,1)} %bitcast.34), calls=%async_computation.3 | async-start | bytes 1048576
  3.5 43.8 %slice-start.5 = ((s8[4718592]{0:T(1024)(128)(4,1)}), s8[524288]{0:T(1024)(128)(4,1)S(1)}, s32[]{:S(2)}) async-start(s8[4718592]{0:T(1024)(128)(4,1)} %bitcast.37), calls=%async_computation.5 | async-start | bytes 1048576
  3.5 43.8 %copy-start.15 = (f32[2,512]{1,0:T(2,128)S(1)}, f32[2,512]{1,0:T(2,128)}, u32[]{:S(2)}) copy-start(f32[2,512]{1,0:T(2,128)} %refs_2_.5) | copy-start | bytes 12292
  3.5 43.8 %copy-start.16 = (f32[2,512]{1,0:T(2,128)S(1)}, f32[2,512]{1,0:T(2,128)}, u32[]{:S(2)}) copy-start(f32[2,512]{1,0:T(2,128)} %refs_4_.4) | copy-start | bytes 12292
  25.8 38.8 %slice-start.6 = ((s8[4718592]{0:T(1024)(128)(4,1)}), s8[4194304]{0:T(1024)(128)(4,1)S(1)}, s32[]{:S(2)}) async-start(s8[4718592]{0:T(1024)(128)(4,1)} %bitcast.41), calls=%async_computation.6 | async-start | bytes 8388608
  25.8 38.8 %slice-start.8 = ((s8[4718592]{0:T(1024)(128)(4,1)}), s8[4194304]{0:T(1024)(128)(4,1)S(1)}, s32[]{:S(2)}) async-start(s8[4718592]{0:T(1024)(128)(4,1)} %bitcast.44), calls=%async_computation.8 | async-start | bytes 8388608
  47.3 17.3 %slice-start.7 = ((s8[4718592]{0:T(1024)(128)(4,1)}), s8[524288]{0:T(1024)(128)(4,1)S(1)}, s32[]{:S(2)}) async-start(s8[4718592]{0:T(1024)(128)(4,1)} %bitcast.41), calls=%async_computation.7 | async-start | bytes 1048576
  47.3 17.3 %slice-start.9 = ((s8[4718592]{0:T(1024)(128)(4,1)}), s8[524288]{0:T(1024)(128)(4,1)S(1)}, s32[]{:S(2)}) async-start(s8[4718592]{0:T(1024)(128)(4,1)} %bitcast.44), calls=%async_computation.9 | async-start | bytes 1048576
  47.3 17.3 %copy-start = (bf16[3,3,512,512]{3,2,1,0:T(8,128)(2,1)S(1)}, bf16[3,3,512,512]{3,2,1,0:T(8,128)(2,1)}, u32[]{:S(2)}) copy-start(bf16[3,3,512,512]{3,2,1,0:T(8,128)(2,1)} %param.52) | copy-start | bytes 14155780
  47.3 17.3 %copy-start.17 = (f32[2,512]{1,0:T(2,128)S(1)}, f32[2,512]{1,0:T(2,128)}, u32[]{:S(2)}) copy-start(f32[2,512]{1,0:T(2,128)} %refs_2_.6) | copy-start | bytes 12292
  47.4 17.3 %copy-start.18 = (f32[2,512]{1,0:T(2,128)S(1)}, f32[2,512]{1,0:T(2,128)}, u32[]{:S(2)}) copy-start(f32[2,512]{1,0:T(2,128)} %refs_4_.5) | copy-start | bytes 12292
  64.7 32.6 %copy-start.1 = (bf16[3,3,512,256]{3,2,1,0:T(8,128)(2,1)S(1)}, bf16[3,3,512,256]{3,2,1,0:T(8,128)(2,1)}, u32[]{:S(2)}) copy-start(bf16[3,3,512,256]{3,2,1,0:T(8,128)(2,1)} %param.54) | copy-start | bytes 7077892
  64.7 32.6 %copy-start.3 = (bf16[3,3,256,256]{3,2,1,0:T(8,128)(2,1)S(1)}, bf16[3,3,256,256]{3,2,1,0:T(8,128)(2,1)}, u32[]{:S(2)}) copy-start(bf16[3,3,256,256]{3,2,1,0:T(8,128)(2,1)} %param.56) | copy-start | bytes 3538948
  64.7 32.6 %copy-start.4 = (bf16[3,3,256,256]{3,2,1,0:T(8,128)(2,1)S(1)}, bf16[3,3,256,256]{3,2,1,0:T(8,128)(2,1)}, u32[]{:S(2)}) copy-start(bf16[3,3,256,256]{3,2,1,0:T(8,128)(2,1)} %param.58) | copy-start | bytes 3538948
  64.7 32.6 %copy-start.8 = (bf16[512,256]{1,0:T(8,128)(2,1)S(1)}, bf16[512,256]{1,0:T(8,128)(2,1)}, u32[]{:S(2)}) copy-start(bf16[512,256]{1,0:T(8,128)(2,1)} %refs_4_.6) | copy-start | bytes 786436
  64.8 32.5 %copy-start.13 = (f32[2,512]{1,0:T(2,128)S(1)}, f32[2,512]{1,0:T(2,128)}, u32[]{:S(2)}) copy-start(f32[2,512]{1,0:T(2,128)} %refs_2_.7) | copy-start | bytes 12292
  64.8 32.5 %copy-start.19 = (f32[2,256]{1,0:T(2,128)S(1)}, f32[2,256]{1,0:T(2,128)}, u32[]{:S(2)}) copy-start(f32[2,256]{1,0:T(2,128)} %refs_5_.1) | copy-start | bytes 6148
  97.3 41.2 %copy-start.5 = (bf16[3,3,256,128]{3,2,1,0:T(8,128)(2,1)S(1)}, bf16[3,3,256,128]{3,2,1,0:T(8,128)(2,1)}, u32[]{:S(2)}) copy-start(bf16[3,3,256,128]{3,2,1,0:T(8,128)(2,1)} %param.60) | copy-start | bytes 1769476
  97.3 41.2 %copy-start.11 = (bf16[256,128]{1,0:T(8,128)(2,1)S(1)}, bf16[256,128]{1,0:T(8,128)(2,1)}, u32[]{:S(2)}) copy-start(bf16[256,128]{1,0:T(8,128)(2,1)} %refs_4_.7) | copy-start | bytes 196612
  97.3 41.2 %copy-start.20 = (f32[2,256]{1,0:T(2,128)S(1)}, f32[2,256]{1,0:T(2,128)}, u32[]{:S(2)}) copy-start(f32[2,256]{1,0:T(2,128)} %refs_2_.8) | copy-start | bytes 6148
  138.6 22.8 %copy-start.7 = (bf16[3,3,128,128]{3,2,1,0:T(8,128)(2,1)S(1)}, bf16[3,3,128,128]{3,2,1,0:T(8,128)(2,1)}, u32[]{:S(2)}) copy-start(bf16[3,3,128,128]{3,2,1,0:T(8,128)(2,1)} %param.62) | copy-start | bytes 884740
  138.6 22.8 %copy-start.21 = (f32[2,128]{1,0:T(2,128)S(1)}, f32[2,128]{1,0:T(2,128)}, u32[]{:S(2)}) copy-start(f32[2,128]{1,0:T(2,128)} %refs_2_.9) | copy-start | bytes 3076
  161.4 15.9 %copy-start.23 = (bf16[3,3,128,3]{2,3,1,0:T(4,128)(2,1)S(1)}, bf16[3,3,128,3]{2,3,1,0:T(4,128)(2,1)}, u32[]{:S(2)}) copy-start(bf16[3,3,128,3]{2,3,1,0:T(4,128)(2,1)} %param.65) | copy-start | bytes 20740
  161.4 15.9 %copy-start.22 = (f32[2,128]{1,0:T(2,128)S(1)}, f32[2,128]{1,0:T(2,128)}, u32[]{:S(2)}) copy-start(f32[2,128]{1,0:T(2,128)} %norm_ref.3) | copy-start | bytes 3076
